TPU v7x, 8 devices: a whole 2x2x1 slice. The times are simulated.
8 devices in a mesh: dp: 1 (over z), x: 8 (over y, x, core).
Axes of the slice: x: 2, y: 2, z: 1, core: 2. Of those that a mesh axis runs over, the one named last changes fastest.
Arguments:
- start_pos: int32 [256], P('dp')
- hidden_in: bfloat16 [4, 256, 5120], P(None, ('dp', 'x'))
- k_cache: bfloat16 [256, 256, 8, 128], P('dp', None, 'x')
- v_cache: bfloat16 [256, 256, 8, 128], P('dp', None, 'x')
- attn_norm: bfloat16 [5120], replicated
- w_q: bfloat16 [5120, 5120], replicated
- w_k: bfloat16 [5120, 1024], replicated
- w_v: bfloat16 [5120, 1024], replicated
- q_norm: bfloat16 [128], replicated
- k_norm: bfloat16 [128], replicated
- w_o: bfloat16 [5120, 5120], replicated
- mlp_norm: bfloat16 [5120], replicated
- w_gate: bfloat16 [5120, 17408], replicated
- w_up: bfloat16 [5120, 17408], replicated
- w_down: bfloat16 [17408, 5120], replicated
Outputs:
- output 1: bfloat16 [4, 256, 5120], P(None, ('dp', 'x'))
- output 2: bfloat16 [256, 256, 8, 128], P(('dp', 'x'))
- output 3: bfloat16 [256, 256, 8, 128], P(('dp', 'x'))
All inputs are finite; a program needn't handle non-finite values.
Results may differ from a plain program's by a relative error of at most 0.0104501.
Values are sent between devices in bfloat16 or wider.
A program may use at most 2.75 GiB of HBM per device.

v0:
```python
import jax
import jax.numpy as jnp
from jax import lax
from jax.sharding import PartitionSpec as P

EPS = 1e-6
THETA = 1000000.0


def rms_norm(values, gain_vec):
    values32 = values.astype(jnp.float32)
    inv_rms = lax.rsqrt(jnp.mean(values32 * values32, axis=-1, keepdims=True) + EPS)
    return values32 * inv_rms * gain_vec.astype(jnp.float32)


def rotary(values, positions):
    head_dim = values.shape[-1]
    half_dim = head_dim // 2
    inv_freq = jnp.power(THETA, -jnp.arange(half_dim, dtype=jnp.float32) * 2.0 / head_dim)
    angles = positions.astype(jnp.float32)[..., None, None] * inv_freq
    cos_part = jnp.cos(angles)
    sin_part = jnp.sin(angles)
    first_half = values[..., :half_dim]
    second_half = values[..., half_dim:]
    return jnp.concatenate([first_half * cos_part - second_half * sin_part, second_half * cos_part + first_half * sin_part], axis=-1)


def project(hidden, positions, attn_norm, w_q, w_k, w_v, q_norm, k_norm):
    n_steps, num_rows = hidden.shape[0], hidden.shape[1]
    head_dim = q_norm.shape[0]
    normed = rms_norm(hidden, attn_norm).astype(jnp.bfloat16)
    queries = jnp.einsum('sbd,de->sbe', normed, w_q, preferred_element_type=jnp.float32).reshape(n_steps, num_rows, -1, head_dim)
    keys_new = jnp.einsum('sbd,de->sbe', normed, w_k, preferred_element_type=jnp.float32).reshape(n_steps, num_rows, -1, head_dim)
    values_new = jnp.einsum('sbd,de->sbe', normed, w_v, preferred_element_type=jnp.float32).reshape(n_steps, num_rows, -1, head_dim)
    queries = rotary(rms_norm(queries, q_norm), positions).astype(jnp.bfloat16)
    keys_new = rotary(rms_norm(keys_new, k_norm), positions).astype(jnp.bfloat16)
    return queries, keys_new, values_new.astype(jnp.bfloat16)


def attend(queries, cache_k, cache_v, keys_new, values_new, start_pos):
    n_steps, num_rows, n_heads, head_dim = queries.shape
    num_slots, kv_local = cache_k.shape[1], cache_k.shape[2]
    grouped = queries.reshape(n_steps, num_rows, kv_local, n_heads // kv_local, head_dim)
    score_scale = head_dim ** -0.5
    old_scores = jnp.einsum('sbkgd,btkd->bkgst', grouped, cache_k, preferred_element_type=jnp.float32) * score_scale
    old_valid = (jnp.arange(num_slots)[None, :] < start_pos[:, None])[:, None, None, None, :]
    old_scores = jnp.where(old_valid, old_scores, -jnp.inf)
    new_scores = jnp.einsum('sbkgd,jbkd->bkgsj', grouped, keys_new, preferred_element_type=jnp.float32) * score_scale
    new_valid = jnp.arange(n_steps)[:, None] >= jnp.arange(n_steps)[None, :]
    new_scores = jnp.where(new_valid, new_scores, -jnp.inf)
    peak_score = jnp.maximum(jnp.max(old_scores, axis=-1, keepdims=True), jnp.max(new_scores, axis=-1, keepdims=True))
    old_weights = jnp.exp(old_scores - peak_score)
    new_weights = jnp.exp(new_scores - peak_score)
    weight_sum = jnp.sum(old_weights, axis=-1) + jnp.sum(new_weights, axis=-1)
    mixed_vals = jnp.einsum('bkgst,btkd->sbkgd', old_weights.astype(jnp.bfloat16), cache_v, preferred_element_type=jnp.float32)
    mixed_vals = mixed_vals + jnp.einsum('bkgsj,jbkd->sbkgd', new_weights.astype(jnp.bfloat16), values_new, preferred_element_type=jnp.float32)
    mixed_vals = mixed_vals / jnp.transpose(weight_sum, (3, 0, 1, 2))[..., None]
    return mixed_vals.astype(jnp.bfloat16).reshape(n_steps, num_rows, n_heads, head_dim)


def finish(hidden, attended, w_o, mlp_norm, w_gate, w_up, w_down):
    n_steps, num_rows = attended.shape[0], attended.shape[1]
    flat_attn = attended.reshape(n_steps, num_rows, -1)
    attn_out = jnp.einsum('sbe,ed->sbd', flat_attn, w_o, preferred_element_type=jnp.float32)
    residual = (hidden.astype(jnp.float32) + attn_out).astype(jnp.bfloat16)
    normed = rms_norm(residual, mlp_norm).astype(jnp.bfloat16)
    gate_val = jnp.einsum('sbd,df->sbf', normed, w_gate, preferred_element_type=jnp.float32)
    up_val = jnp.einsum('sbd,df->sbf', normed, w_up, preferred_element_type=jnp.float32)
    activated = (jax.nn.silu(gate_val) * up_val).astype(jnp.bfloat16)
    down_val = jnp.einsum('sbf,fd->sbd', activated, w_down, preferred_element_type=jnp.float32)
    return (residual.astype(jnp.float32) + down_val).astype(jnp.bfloat16)


def write_slots(cache_arr, fresh_rows, start_pos):
    slot_ids = jnp.arange(cache_arr.shape[1])[None, :, None, None]
    for step_idx in range(fresh_rows.shape[0]):
        slot_hit = slot_ids == (start_pos + step_idx)[:, None, None, None]
        cache_arr = jnp.where(slot_hit, fresh_rows[step_idx][:, None], cache_arr)
    return cache_arr


def solution(mesh):
    row_spec = P(None, ('dp', 'x'), None)
    cache_in = P('dp', None, 'x', None)
    cache_out = P(('dp', 'x'), None, None, None)

    def local_run(start_pos, hidden_in, k_heads, v_heads, attn_norm, w_q, w_k, w_v, q_norm, k_norm, w_o, mlp_norm, w_gate, w_up, w_down):
        num_rows = hidden_in.shape[1]
        my_pos = lax.dynamic_slice_in_dim(start_pos, lax.axis_index('x') * num_rows, num_rows)
        k_local = lax.all_to_all(k_heads, 'x', 0, 2, tiled=True)
        v_local = lax.all_to_all(v_heads, 'x', 0, 2, tiled=True)
        positions = my_pos[None, :] + jnp.arange(hidden_in.shape[0])[:, None]
        queries, keys_new, values_new = project(hidden_in, positions, attn_norm, w_q, w_k, w_v, q_norm, k_norm)
        attended = attend(queries, k_local, v_local, keys_new, values_new, my_pos)
        out_hidden = finish(hidden_in, attended, w_o, mlp_norm, w_gate, w_up, w_down)
        return out_hidden, write_slots(k_local, keys_new, my_pos), write_slots(v_local, values_new, my_pos)

    return jax.shard_map(local_run, mesh=mesh, in_specs=(P('dp'), row_spec, cache_in, cache_in) + (P(),) * 11, out_specs=(row_spec, cache_out, cache_out), check_vma=False)
```

profile of v0, /device:TPU:0, one launch (start us, length us, event | category | flops | bytes accessed | tf_op | source)
XLA Modules:
  0.0 652.9 jit_solution(13060341130518597092)
XLA Ops:
  0.6 191.0 %all_to_all.36 = bf16[256,256,1,128]{3,1,2,0:T(8,128)(2,1)} all-to-all(bf16[256,256,1,128]{3,1,2,0:T(8,128)(2,1)} %param.17), channel_id=1, replica_groups=mesh['dp'=1,'x'=8] {'x'}, dimensions={0} | all-to-all | bytes 33554432 | tf_op jit(solution)/shard_map/all_to_all | solution.py:90
  191.6 4.6 all-to-all-start.1
  196.3 0.4 fusion.69
  196.6 18.1 %fusion.8 = f32[4,32,5120]{2,1,0:T(8,128)S(1)} fusion(bf16[5120,5120]{1,0:T(8,128)(2,1)} %param.20, bf16[4,32,5120]{2,1,0:T(8,128)(2,1)S(1)} %copy-done.1, f32[5120]{0:T(1024)S(1)} %convert_element_type.62, f32[4,32]{1,0:T(4,128)S(1)} %add_rsqrt_fusion.3), kind=kOutput, calls=%fused_computation.8 | convolution fusion | flops 6713507840 | bytes 56381952 | tf_op jit(solution)/shard_map/sbd,de->sbe/dot_general | solution.py:32
  214.8 0.0 copy-start.2
  214.8 0.5 copy.78
  215.3 1.0 copy-done.2
  216.3 0.7 fusion.72
  217.1 0.1 copy.52
  217.2 0.1 broadcast_add_fusion.2
  217.3 0.1 add_convert_fusion.2
  217.3 0.5 multiply_cosine_fusion
  217.9 2.3 fusion.73
  220.3 0.0 copy-done.8
  220.3 0.9 subtract_convert_fusion
  221.2 0.7 copy.57
  221.9 2.0 copy.56
  223.9 5.6 fusion.32
  229.4 0.1 copy.79
  229.6 0.0 copy-start.5
  229.6 0.8 copy-done.5
  230.4 0.8 multiply_reduce_fusion.1
  231.2 0.9 copy.59
  232.1 0.8 copy.60
  232.9 5.6 fusion.82
  238.6 0.0 copy-done.20
  238.7 0.6 copy.84
  239.3 0.6 copy.83
  239.9 0.6 copy.82
  240.5 0.6 copy.81
  241.2 0.0 copy-done.6
  241.2 0.0 copy-start.4
  241.2 0.4 fusion.90
  241.7 0.5 subtract_convert_fusion.1
  242.2 1.2 slice_maximum_fusion.3
  243.4 0.1 iota_compare_fusion.1
  243.5 0.1 iota_compare_fusion
  243.6 0.6 copy_bitcast_fusion
  244.2 0.7 copy_bitcast_fusion.2
  244.9 0.7 bitcast_bitcast_fusion
  245.6 0.0 copy-done.4
  245.6 11.6 %fusion.99 = (f32[32,8,5,4]{2,3,1,0:T(4,128)S(1)}, f32[32,8,5,4,4]{2,4,3,1,0:T(4,128)}) fusion(bf16[4,32,8,5,64]{4,3,0,2,1:T(8,128)(2,1)S(1)} %copy.57, bf16[4,32,8,5,64]{4,3,0,2,1:T(8,128)(2,1)S(1)} %copy-done.4, bf16[4,32,8,64]{3,0,2,1:T(4,128)(2,1)S(1)} %get-tuple-element.20, bf16[4,32,8,64]{3,0,2,1:T(4,128)(2,1)S(1)} %get-tuple-element.19, ...), kind=kOutput, calls=%fused_computation.123 | convolution fusion | flops 8444928 | bytes 1675280 | tf_op jit(solution)/shard_map/sbkgd,jbkd->bkgsj/dot_general | solution.py:48
  257.2 11.2 %bitcast_reduce_fusion = (f32[32,8,5,4]{2,3,1,0:T(4,128)S(1)}, f32[32,8,4,5,256]{4,3,2,1,0:T(8,128)}) fusion(pred[32,256]{1,0:T(8,128)(4,1)S(1)} %get-tuple-element.36, bf16[8,32,256,1,128]{4,2,1,0,3:T(8,128)(2,1)} %bitcast.172, bf16[4,32,8,5,64]{4,3,0,2,1:T(8,128)(2,1)S(1)} %copy.57, bf16[4,32,8,5,64]{4,3,0,2,1:T(8,128)(2,1)} %copy.56), kind=kOutput, calls=%fused_computation.36 | convolution fusion | flops 342092800 | bytes 23359488 | tf_op jit(solution)/shard_map/sbkgd,btkd->bkgst/dot_general | solution.py:45
  268.4 0.2 max.8
  268.6 5.5 fusion.40
  274.1 106.0 %all-to-all-done.1 = bf16[256,256,1,128]{3,1,2,0:T(8,128)(2,1)} async-done(((bf16[256,256,1,128]{3,1,2,0:T(8,128)(2,1)}), bf16[256,256,1,128]{3,1,2,0:T(8,128)(2,1)}, u32[]{:S(2)}, u32[]{:S(2)}) %all-to-all-start.1) | async-done | bytes 16777248 | tf_op jit(solution)/shard_map/all_to_all | solution.py:91
  380.2 10.2 %fusion.18 = f32[32,8,5,4,128]{4,2,3,1,0:T(8,128)S(1)} fusion(bf16[8,32,256,1,128]{4,2,1,0,3:T(8,128)(2,1)} %bitcast.13, f32[32,8,4,5,256]{4,3,2,1,0:T(8,128)} %get-tuple-element.38, f32[32,8,5,4]{2,3,1,0:T(4,128)S(1)} %max.8, pred[32,256]{1,0:T(8,128)(4,1)S(1)} %get-tuple-element.36), kind=kOutput, calls=%fused_computation.12 | convolution fusion | flops 340787200 | bytes 24670208 | tf_op jit(solution)/shard_map/bkgst,btkd->sbkgd/dot_general | solution.py:55
  390.4 0.0 copy-start.11
  390.4 1.9 fusion.74
  392.3 0.2 add_bitcast_fusion
  392.5 2.8 fusion.64
  395.3 0.6 copy.64
  395.9 2.3 reshape_reshape.3
  398.2 0.0 copy-start.16
  398.2 0.0 copy-start.17
  398.2 0.0 copy-start.18
  398.2 20.9 %multiply_reduce_fusion = (f32[4,32]{1,0:T(4,128)S(1)}, f32[4,32,5120]{2,1,0:T(8,128)}) fusion(bf16[4,32,5120]{2,1,0:T(8,128)(2,1)} %reshape_reshape.3, bf16[5120,5120]{1,0:T(8,128)(2,1)} %param.25, bf16[4,32,5120]{2,1,0:T(8,128)(2,1)S(1)} %copy-done.1), kind=kOutput, calls=%fused_computation.64 | convolution fusion | flops 6714818560 | bytes 57672192 | tf_op jit(solution)/shard_map/sbe,ed->sbd/dot_general | solution.py:64
  419.2 23.0 %fusion.24 = (bf16[32,256,8,128]{3,1,2,0:T(8,128)(2,1)}, bf16[32,256,8,128]{3,1,2,0:T(8,128)(2,1)}) fusion(pred[32,256]{1,0:T(8,128)(4,1)S(1)} %get-tuple-element.35, pred[32,256]{1,0:T(8,128)(4,1)S(1)} %get-tuple-element.44, pred[32,256]{1,0:T(8,128)(4,1)S(1)} %get-tuple-element.45, pred[32,256]{1,0:T(8,128)(4,1)S(1)} %get-tuple-element.43, ...), kind=kLoop, calls=%fused_computation.19 | loop fusion | flops 67108864 | bytes 67665920 | tf_op jit(solution)/shard_map/jit(_where)/select_n | solution.py:78
  442.2 0.0 copy-start
  442.2 20.0 %copy.65 = bf16[32,256,8,128]{3,2,1,0:T(8,128)(2,1)} copy(bf16[32,256,8,128]{3,1,2,0:T(8,128)(2,1)} %get-tuple-element.30) | data formatting | bytes 33554432
  462.2 12.1 %copy.66 = bf16[32,256,8,128]{3,2,1,0:T(8,128)(2,1)} copy(bf16[32,256,8,128]{3,1,2,0:T(8,128)(2,1)S(1)} %copy-done) | data formatting | bytes 33554432
  474.3 59.8 %fusion.4 = f32[4,32,17408]{2,1,0:T(8,128)} fusion(bf16[5120,17408]{1,0:T(8,128)(2,1)} %param.27, f32[4,32,5120]{2,1,0:T(8,128)S(1)} %copy-done.3, f32[5120]{0:T(1024)S(1)} %convert_element_type.74, f32[4,32]{1,0:T(4,128)S(1)} %add_rsqrt_fusion.2), kind=kOutput, calls=%fused_computation.4 | convolution fusion | flops 22818979840 | bytes 189813248 | tf_op jit(solution)/shard_map/sbd,df->sbf/dot_general | solution.py:67
  534.1 60.5 %fusion.13.clone.8 = bf16[4,32,17408]{2,1,0:T(8,128)(2,1)} fusion(bf16[5120,17408]{1,0:T(8,128)(2,1)} %param.28, f32[4,32,17408]{2,1,0:T(8,128)} %fusion.4, f32[4,32,5120]{2,1,0:T(8,128)S(1)} %copy-done.3, f32[5120]{0:T(1024)S(1)} %convert_element_type.74, f32[4,32]{1,0:T(4,128)S(1)} %add_rsqrt_fusion.2), kind=kOutput, calls=%fused_computation.11.clone.clone.clone.clone.clone.clone.clone.1 | convolution fusion | flops 22832349184 | bytes 194269696 | tf_op jit(solution)/shard_map/sbd,df->sbf/dot_general | solution.py:68
  594.6 58.1 %fusion.56 = bf16[4,32,5120]{2,1,0:T(8,128)(2,1)} fusion(f32[4,32,5120]{2,1,0:T(8,128)S(1)} %copy-done.3, bf16[17408,5120]{1,0:T(8,128)(2,1)} %param.29, bf16[4,32,17408]{2,1,0:T(8,128)(2,1)} %fusion.13.clone.8), kind=kOutput, calls=%fused_computation.45 | convolution fusion | flops 22818324480 | bytes 186646528 | tf_op jit(solution)/shard_map/sbf,fd->sbd/dot_general | solution.py:70
  (49 shorter events, 0.2 us)
Async XLA Ops:
  191.6 4.6 copy-start.22
  191.6 4.7 copy-start.19
  191.6 4.7 copy-start.1
  191.6 188.6 %all-to-all-start.1 = ((bf16[256,256,1,128]{3,1,2,0:T(8,128)(2,1)}), bf16[256,256,1,128]{3,1,2,0:T(8,128)(2,1)}, u32[]{:S(2)}, u32[]{:S(2)}) async-start(bf16[256,256,1,128]{3,1,2,0:T(8,128)(2,1)} %param.18), calls=%async_computation.1 | async-start | bytes 33554432 | tf_op jit(solution)/shard_map/all_to_all | solution.py:91
  214.8 1.5 copy-start.2
  216.3 0.9 copy-start.21
  217.9 2.4 copy-start.8
  223.9 5.7 copy-start.23
  229.6 0.8 copy-start.5
  232.9 5.7 copy-start.20
  232.9 8.3 %copy-start.6 = (f32[16,8,8,128]{3,2,1,0:T(8,128)S(1)}, f32[16,8,8,128]{3,2,1,0:T(8,128)}, u32[]{:S(2)}) copy-start(f32[16,8,8,128]{3,2,1,0:T(8,128)} %copy-done.5) | copy-start | bytes 1572868
  232.9 8.3 %copy-start.10 = (f32[4,32,8]{0,2,1:T(8,128)S(1)}, f32[4,32,8]{0,2,1:T(8,128)}, u32[]{:S(2)}) copy-start(f32[4,32,8]{0,2,1:T(8,128)} %copy.60) | copy-start | bytes 12292
  238.5 3.1 copy-start.9
  241.2 4.4 copy-start.4
  380.2 10.3 %copy-start.7 = (f32[32,8,5,4,4]{2,4,3,1,0:T(4,128)S(1)}, f32[32,8,5,4,4]{2,4,3,1,0:T(4,128)}, u32[]{:S(2)}) copy-start(f32[32,8,5,4,4]{2,4,3,1,0:T(4,128)} %get-tuple-element.40) | copy-start | bytes 245764
  390.4 2.1 copy-start.11
  398.2 20.9 %copy-start.12 = (bf16[4,8,8,128]{3,2,1,0:T(8,128)(2,1)S(1)}, bf16[4,8,8,128]{3,2,1,0:T(8,128)(2,1)}, u32[]{:S(2)}) copy-start(bf16[4,8,8,128]{3,2,1,0:T(8,128)(2,1)} %copy.84) | copy-start | bytes 196612
  398.2 20.9 %copy-start.13 = (bf16[4,8,8,128]{3,2,1,0:T(8,128)(2,1)S(1)}, bf16[4,8,8,128]{3,2,1,0:T(8,128)(2,1)}, u32[]{:S(2)}) copy-start(bf16[4,8,8,128]{3,2,1,0:T(8,128)(2,1)} %copy.83) | copy-start | bytes 196612
  398.2 20.9 %copy-start.14 = (bf16[4,8,8,128]{3,2,1,0:T(8,128)(2,1)S(1)}, bf16[4,8,8,128]{3,2,1,0:T(8,128)(2,1)}, u32[]{:S(2)}) copy-start(bf16[4,8,8,128]{3,2,1,0:T(8,128)(2,1)} %copy.82) | copy-start | bytes 196612
  398.2 20.9 %copy-start.15 = (bf16[4,8,8,128]{3,2,1,0:T(8,128)(2,1)S(1)}, bf16[4,8,8,128]{3,2,1,0:T(8,128)(2,1)}, u32[]{:S(2)}) copy-start(bf16[4,8,8,128]{3,2,1,0:T(8,128)(2,1)} %copy.81) | copy-start | bytes 196612
  398.2 21.0 %copy-start.16 = (bf16[32,8,128]{2,1,0:T(8,128)(2,1)S(1)}, bf16[32,8,128]{2,1,0:T(8,128)(2,1)}, u32[]{:S(2)}) copy-start(bf16[32,8,128]{2,1,0:T(8,128)(2,1)} %get-tuple-element.47) | copy-start | bytes 196612
  398.2 21.0 %copy-start.17 = (bf16[32,8,128]{2,1,0:T(8,128)(2,1)S(1)}, bf16[32,8,128]{2,1,0:T(8,128)(2,1)}, u32[]{:S(2)}) copy-start(bf16[32,8,128]{2,1,0:T(8,128)(2,1)} %get-tuple-element.48) | copy-start | bytes 196612
  398.2 21.0 %copy-start.18 = (bf16[32,8,128]{2,1,0:T(8,128)(2,1)S(1)}, bf16[32,8,128]{2,1,0:T(8,128)(2,1)}, u32[]{:S(2)}) copy-start(bf16[32,8,128]{2,1,0:T(8,128)(2,1)} %get-tuple-element.49) | copy-start | bytes 196612
  442.2 20.0 %copy-start = (bf16[32,256,8,128]{3,1,2,0:T(8,128)(2,1)S(1)}, bf16[32,256,8,128]{3,1,2,0:T(8,128)(2,1)}, u32[]{:S(2)}) copy-start(bf16[32,256,8,128]{3,1,2,0:T(8,128)(2,1)} %get-tuple-element.29) | copy-start | bytes 50331652
  462.2 12.1 %copy-start.3 = (f32[4,32,5120]{2,1,0:T(8,128)S(1)}, f32[4,32,5120]{2,1,0:T(8,128)}, u32[]{:S(2)}) copy-start(f32[4,32,5120]{2,1,0:T(8,128)} %get-tuple-element.42) | copy-start | bytes 7864324
where the time goes:
time: 657 us; the launch traced here: 653 us
  matrix products  264 us (40%)
  blocking collectives  191 us (29%)
  waiting for transfers between devices  106 us (16%)
  local copies, waits for them, and re-layouts  46.6 us (7%)
  other arithmetic  39 us (6%)
    all_to_all x1, blocking collectives, local_run(): k_local = lax.all_to_all(k_heads, 'x', 0, 2, tiled=True)  191 us
    all_to_all x1, waiting for transfers between devices, local_run(): v_local = lax.all_to_all(v_heads, 'x', 0, 2, tiled=True)  106 us
    dot_general x1, matrix products, finish(): jnp.einsum('sbd,df->sbf', normed, w_up, preferred_element_type=jnp.float32)  60.5 us
    dot_general x1, matrix products, finish(): jnp.einsum('sbd,df->sbf', normed, w_gate, preferred_element_type=jnp.floa...  59.8 us
    dot_general x1, matrix products, finish(): jnp.einsum('sbf,fd->sbd', activated, w_down, preferred_element_type=jnp.f...  58.1 us
    unnamed x60, local copies, waits for them, and re-layouts  38.5 us
    select_n x1, other arithmetic, write_slots(): cache_arr = jnp.where(slot_hit, fresh_rows[step_idx][:, None], cache_arr)  23 us
    dot_general x1, matrix products, finish(): jnp.einsum('sbe,ed->sbd', flat_attn, w_o, preferred_element_type=jnp.floa...  20.9 us
  transfers between devices with their start and end apart: 1, of which 1 were waited for; matrix products, arithmetic and copies ran while one was open for 12% of the time, Pallas kernels for 0%

commit v1 on v0

--- a/solution.py
+++ b/solution.py
@@ -1,6 +1,8 @@
 import jax
 import jax.numpy as jnp
 from jax import lax
+from jax.experimental import pallas as pl
+from jax.experimental.pallas import tpu as pltpu
 from jax.sharding import PartitionSpec as P
 
 EPS = 1e-6
@@ -71,28 +73,71 @@
     return (residual.astype(jnp.float32) + down_val).astype(jnp.bfloat16)
 
 
-def write_slots(cache_arr, fresh_rows, start_pos):
-    slot_ids = jnp.arange(cache_arr.shape[1])[None, :, None, None]
-    for step_idx in range(fresh_rows.shape[0]):
-        slot_hit = slot_ids == (start_pos + step_idx)[:, None, None, None]
-        cache_arr = jnp.where(slot_hit, fresh_rows[step_idx][:, None], cache_arr)
-    return cache_arr
+def merge_kernel(pos_ref, blocks_ref, fresh_ref, out_ref, wide_ref):
+    num_heads = blocks_ref.shape[0]
+    for head_idx in range(num_heads):
+        wide_ref[:, head_idx, :] = blocks_ref[head_idx, 0].astype(jnp.float32)
+    out_ref[0] = wide_ref[...].astype(out_ref.dtype)
+    first_slot = pos_ref[pl.program_id(0)]
+    for step_idx in range(fresh_ref.shape[0]):
+        out_ref[0, first_slot + step_idx] = fresh_ref[step_idx, 0]
+
+
+def merge_heads(blocks, fresh_rows, start_pos):
+    num_heads, num_rows, num_slots, head_dim = blocks.shape
+    n_steps = fresh_rows.shape[0]
+    return pl.pallas_call(
+        merge_kernel,
+        out_shape=jax.ShapeDtypeStruct((num_rows, num_slots, num_heads, head_dim), blocks.dtype),
+        grid_spec=pltpu.PrefetchScalarGridSpec(
+            num_scalar_prefetch=1,
+            grid=(num_rows,),
+            in_specs=[
+                pl.BlockSpec((num_heads, 1, num_slots, head_dim), lambda b, pos: (0, b, 0, 0)),
+                pl.BlockSpec((n_steps, 1, num_heads, head_dim), lambda b, pos: (0, b, 0, 0)),
+            ],
+            out_specs=pl.BlockSpec((1, num_slots, num_heads, head_dim), lambda b, pos: (b, 0, 0, 0)),
+            scratch_shapes=[pltpu.VMEM((num_slots, num_heads, head_dim), jnp.float32)],
+        ),
+        cost_estimate=pl.CostEstimate(flops=10**9, bytes_accessed=2 * blocks.size * 2, transcendentals=0),
+    )(start_pos, blocks, fresh_rows)
 
 
 def solution(mesh):
+    n_dev = mesh.shape['x']
     row_spec = P(None, ('dp', 'x'), None)
     cache_in = P('dp', None, 'x', None)
     cache_out = P(('dp', 'x'), None, None, None)
 
+    def swap(arr):
+        return lax.all_to_all(arr, 'x', 0, 0, tiled=True)
+
     def local_run(start_pos, hidden_in, k_heads, v_heads, attn_norm, w_q, w_k, w_v, q_norm, k_norm, w_o, mlp_norm, w_gate, w_up, w_down):
-        num_rows = hidden_in.shape[1]
+        n_steps, num_rows, _ = hidden_in.shape
+        all_rows, num_slots, _, head_dim = k_heads.shape
         my_pos = lax.dynamic_slice_in_dim(start_pos, lax.axis_index('x') * num_rows, num_rows)
-        k_local = lax.all_to_all(k_heads, 'x', 0, 2, tiled=True)
-        v_local = lax.all_to_all(v_heads, 'x', 0, 2, tiled=True)
-        positions = my_pos[None, :] + jnp.arange(hidden_in.shape[0])[:, None]
+        k_own, v_own = k_heads[:, :, 0], v_heads[:, :, 0]
+        k_got = swap(k_own).reshape(n_dev, num_rows, num_slots, head_dim)
+        positions = my_pos[None, :] + jnp.arange(n_steps)[:, None]
         queries, keys_new, values_new = project(hidden_in, positions, attn_norm, w_q, w_k, w_v, q_norm, k_norm)
-        attended = attend(queries, k_local, v_local, keys_new, values_new, my_pos)
+        group = queries.shape[2] // n_dev
+        q_send = queries.reshape(n_steps, num_rows, n_dev, group, head_dim).transpose(2, 0, 3, 1, 4).reshape(n_dev, n_steps * group, num_rows, head_dim)
+        k_send = keys_new.transpose(2, 0, 1, 3)
+        v_send = values_new.transpose(2, 0, 1, 3)
+        sent = jnp.concatenate([q_send, k_send, v_send], axis=1)
+        got = swap(sent)
+        got = got.transpose(1, 0, 2, 3).reshape(n_steps * (group + 2), all_rows, head_dim)
+        q_got = got[:n_steps * group].reshape(n_steps, group, all_rows, head_dim).transpose(0, 2, 1, 3)
+        kn_got = got[n_steps * group:n_steps * (group + 1), :, None]
+        vn_got = got[n_steps * (group + 1):, :, None]
+        mixed = attend(q_got, k_heads, v_heads, kn_got, vn_got, start_pos)
+        mixed = mixed.reshape(n_steps, n_dev, num_rows, group, head_dim).transpose(1, 0, 3, 2, 4)
+        v_got = swap(v_own).reshape(n_dev, num_rows, num_slots, head_dim)
+        back = swap(mixed)
+        attended = back.transpose(1, 3, 0, 2, 4).reshape(n_steps, num_rows, n_dev * group, head_dim)
         out_hidden = finish(hidden_in, attended, w_o, mlp_norm, w_gate, w_up, w_down)
-        return out_hidden, write_slots(k_local, keys_new, my_pos), write_slots(v_local, values_new, my_pos)
+        k_out = merge_heads(k_got, keys_new, my_pos)
+        v_out = merge_heads(v_got, values_new, my_pos)
+        return out_hidden, k_out, v_out
 
     return jax.shard_map(local_run, mesh=mesh, in_specs=(P('dp'), row_spec, cache_in, cache_in) + (P(),) * 11, out_specs=(row_spec, cache_out, cache_out), check_vma=False)

time: 657 us -> 560 us (0.85)
  blocking collectives: 191 us -> 0 us
  waiting for transfers between devices: 106 us -> 173 us
  Pallas kernels: 0 us -> 65.4 us
  local copies, waits for them, and re-layouts: 46.6 us -> 13 us
  other arithmetic: 39 us -> 22.5 us
  starting transfers between devices: 4.62 us -> 16.5 us
    all_to_all x1 -> x0, blocking collectives: 191 us -> none  [local_run(): k_local = lax.all_to_all(k_heads, 'x', 0, 2, tiled=True)]
    all_to_all x1 -> x4, waiting for transfers between devices: 106 us -> 173 us  [swap(): return lax.all_to_all(arr, 'x', 0, 0, tiled=True)]
    pallas_call x0 -> x2, Pallas kernels: none -> 65.4 us  [merge_heads(): pl.pallas_call(merge_kernel, out_shape=jax.ShapeDtypeStruct((num_rows, nu...]
    unnamed x60 -> x27, local copies, waits for them, and re-layouts: 38.5 us -> 4.9 us
    select_n x1 -> x0, other arithmetic: 23 us -> none  [write_slots(): cache_arr = jnp.where(slot_hit, fresh_rows[step_idx][:, None], cache_arr)]
    all_to_all x1 -> x4, starting transfers between devices: 4.62 us -> 16.5 us  [swap(): return lax.all_to_all(arr, 'x', 0, 0, tiled=True)]
  transfers between devices with their start and end apart: 1 -> 4, of which waited for: 1 -> 4; matrix products, arithmetic and copies ran while one was open for 12% -> 37% of each run, Pallas kernels for 0% -> 6%
where the time goes in v1:
time: 560 us; the launch traced here: 551 us
  matrix products  259 us (46%)
  waiting for transfers between devices  173 us (31%)
  Pallas kernels  65.4 us (12%)
  other arithmetic  22.5 us (4%)
  starting transfers between devices  16.5 us (3%)
  local copies, waits for them, and re-layouts  13 us (2%)
    all_to_all x4, waiting for transfers between devices, swap(): return lax.all_to_all(arr, 'x', 0, 0, tiled=True)  173 us
    pallas_call x2, Pallas kernels, merge_heads(): pl.pallas_call(merge_kernel, out_shape=jax.ShapeDtypeStruct((num_rows, nu...  65.4 us
    dot_general x1, matrix products, finish(): jnp.einsum('sbd,df->sbf', normed, w_up, preferred_element_type=jnp.float32)  60.5 us
    dot_general x1, matrix products, finish(): jnp.einsum('sbd,df->sbf', normed, w_gate, preferred_element_type=jnp.floa...  59.8 us
    dot_general x1, matrix products, finish(): jnp.einsum('sbf,fd->sbd', activated, w_down, preferred_element_type=jnp.f...  58.1 us
    dot_general x1, matrix products, finish(): jnp.einsum('sbe,ed->sbd', flat_attn, w_o, preferred_element_type=jnp.floa...  20.8 us
    dot_general x1, matrix products, project(): jnp.einsum('sbd,de->sbe', normed, w_q, preferred_element_type=jnp.float32)  18.2 us
    all_to_all x4, starting transfers between devices, swap(): return lax.all_to_all(arr, 'x', 0, 0, tiled=True)  16.5 us
  transfers between devices with their start and end apart: 4, of which 4 were waited for; matrix products, arithmetic and copies ran while one was open for 37% of the time, Pallas kernels for 6%

profile of v1, /device:TPU:0, one launch (start us, length us, event | category | flops | bytes accessed | tf_op | source)
XLA Modules:
  0.0 550.9 jit_solution(16377637897130119218)
XLA Ops:
  0.7 0.7 convert_element_type.63
  1.3 0.7 convert_element_type.65
  2.0 0.8 dynamic_slice.3.pos_ref
  2.7 0.6 copy-done.10
  3.3 1.7 fusion.62
  5.0 0.7 convert_element_type.61
  5.7 6.1 %fusion.82 = bf16[4,32,1024]{2,1,0:T(8,128)(2,1)S(1)} fusion(bf16[5120,1024]{1,0:T(8,128)(2,1)} %param.22, bf16[4,32,5120]{2,1,0:T(8,128)(2,1)} %param.16, f32[5120]{0:T(1024)S(1)} %convert_element_type.61, f32[4,32]{1,0:T(4,128)S(1)} %add_rsqrt_fusion.3), kind=kOutput, calls=%fused_computation.74 | convolution fusion | flops 1344929792 | bytes 12079616 | tf_op jit(solution)/shard_map/sbd,de->sbe/dot_general | solution.py:36
  11.8 0.0 copy-start.6
  11.8 0.7 copy-done.6
  12.6 0.9 copy-done.4
  13.5 1.6 fusion.24
  15.1 0.1 copy.48
  15.2 0.2 fusion.91
  15.5 0.3 multiply_cosine_fusion
  15.8 0.2 fusion.92
  16.0 0.3 subtract_convert_fusion.1
  16.3 0.1 fusion.101
  16.5 18.2 %fusion.8 = f32[4,32,5120]{2,1,0:T(8,128)S(1)} fusion(bf16[5120,5120]{1,0:T(8,128)(2,1)} %param.20, bf16[4,32,5120]{2,1,0:T(8,128)(2,1)S(1)} %copy-done.1, f32[5120]{0:T(1024)S(1)} %convert_element_type.61, f32[4,32]{1,0:T(4,128)S(1)} %add_rsqrt_fusion.3), kind=kOutput, calls=%fused_computation.8 | convolution fusion | flops 6713507840 | bytes 56381952 | tf_op jit(solution)/shard_map/sbd,de->sbe/dot_general | solution.py:34
  34.6 0.0 copy-start.2
  34.6 0.5 copy.47
  35.1 1.0 copy-done.2
  36.1 0.7 fusion.65
  36.9 0.1 copy.31
  37.0 2.2 fusion.66
  39.2 0.9 subtract_convert_fusion
  40.1 0.7 maximum_bitcast_fusion
  40.8 0.3 copy.33
  41.1 1.4 pad_maximum_fusion
  42.6 4.5 all-to-all-start
  47.1 0.0 copy-done.11
  47.1 0.1 iota_compare_fusion
  47.2 23.6 %all-to-all-done = bf16[8,28,32,128]{3,2,1,0:T(8,128)(2,1)S(1)} async-done(((bf16[8,28,32,128]{3,2,1,0:T(8,128)(2,1)}), bf16[8,28,32,128]{3,2,1,0:T(8,128)(2,1)S(1)}, u32[]{:S(2)}, u32[]{:S(2)}) %all-to-all-start) | async-done | bytes 1835040 | tf_op jit(solution)/shard_map/all_to_all | solution.py:113
  70.9 0.3 slice.35
  71.1 0.4 copy.36
  71.5 0.1 copy.39
  71.7 0.1 copy.38
  71.8 10.8 %fusion.97 = (f32[256,5,4]{1,2,0:T(4,128)S(1)}, f32[256,1,5,4,4]{2,4,3,0,1:T(4,128)}) fusion(bf16[4,256,128,1]{2,0,3,1:T(4,128)(2,1)S(1)} %bitcast.212, bf16[4,5,256,128]{3,2,1,0:T(8,128)(2,1)S(1)} %bitcast.195, pred[4,4]{1,0:T(4,128)(4,1)S(1)} %iota_compare_fusion.1), kind=kOutput, calls=%fused_computation.100 | convolution fusion | flops 5299200 | bytes 1675280 | tf_op jit(solution)/shard_map/sbkgd,jbkd->bkgsj/dot_general | solution.py:50
  82.6 12.0 %fusion.34 = (f32[256,5,4]{1,2,0:T(4,128)S(1)}, f32[256,4,5,256]{3,2,1,0:T(8,128)}) fusion(pred[256,256]{1,0:T(8,128)(4,1)S(1)} %iota_compare_fusion, bf16[256,256,1,128]{3,1,2,0:T(8,128)(2,1)} %param.17, bf16[4,5,256,128]{3,2,1,0:T(8,128)(2,1)S(1)} %bitcast.196), kind=kOutput, calls=%fused_computation.30 | convolution fusion | flops 339471360 | bytes 23416832 | tf_op jit(solution)/shard_map/sbkgd,btkd->bkgst/dot_general | solution.py:47
  94.7 0.1 max.8
  94.8 3.6 fusion.74
  98.4 0.0 copy-start
  98.4 6.8 %fusion.32 = f32[256,5,4]{1,2,0:T(4,128)S(1)} fusion(f32[256,4,5,256]{3,2,1,0:T(8,128)} %get-tuple-element.12, f32[256,5,4]{1,2,0:T(4,128)S(1)} %max.8, pred[256,256]{1,0:T(8,128)(4,1)S(1)} %iota_compare_fusion), kind=kLoop, calls=%fused_computation.28 | loop fusion | flops 5237760 | bytes 5349376 | tf_op jit(solution)/shard_map/reduce_sum | solution.py:56
  105.1 0.0 copy-done
  105.2 8.0 %fusion.18 = f32[256,5,4,128]{3,1,2,0:T(8,128)S(1)} fusion(bf16[256,256,1,128]{3,1,2,0:T(8,128)(2,1)} %param.18, f32[256,4,5,256]{3,2,1,0:T(8,128)S(1)} %copy-done, f32[256,5,4]{1,2,0:T(4,128)S(1)} %max.8, pred[256,256]{1,0:T(8,128)(4,1)S(1)} %iota_compare_fusion), kind=kOutput, calls=%fused_computation.12 | convolution fusion | flops 340787200 | bytes 24727552 | tf_op jit(solution)/shard_map/bkgst,btkd->sbkgd/dot_general | solution.py:57
  113.1 0.1 add_bitcast_fusion
  113.3 3.7 fusion.57
  116.9 0.0 copy-start.9
  117.0 1.6 copy.66
  118.6 2.3 all-to-all-start.1
  120.9 0.9 pad_maximum_fusion.1.fresh_ref
  121.8 17.2 %all-to-all-done.1 = bf16[8,4,5,32,128]{4,3,2,1,0:T(8,128)(2,1)S(1)} async-done(((bf16[8,4,5,32,128]{4,3,2,1,0:T(8,128)(2,1)}), bf16[8,4,5,32,128]{4,3,2,1,0:T(8,128)(2,1)S(1)}, u32[]{:S(2)}, u32[]{:S(2)}) %all-to-all-start.1) | async-done | bytes 1310752 | tf_op jit(solution)/shard_map/all_to_all | solution.py:113
  139.0 1.1 copy-done.5
  140.1 4.7 all-to-all-start.3
  144.8 2.0 copy.41
  146.8 2.3 reshape_reshape.7
  149.1 20.8 %multiply_reduce_fusion = (f32[4,32]{1,0:T(4,128)S(1)}, f32[4,32,5120]{2,1,0:T(8,128)}) fusion(bf16[4,32,5120]{2,1,0:T(8,128)(2,1)} %reshape_reshape.7, bf16[5120,5120]{1,0:T(8,128)(2,1)} %param.25, bf16[4,32,5120]{2,1,0:T(8,128)(2,1)S(1)} %copy-done.1), kind=kOutput, calls=%fused_computation.55 | convolution fusion | flops 6714818560 | bytes 57672192 | tf_op jit(solution)/shard_map/sbe,ed->sbd/dot_general | solution.py:66
  169.9 59.8 %fusion.4 = f32[4,32,17408]{2,1,0:T(8,128)} fusion(bf16[5120,17408]{1,0:T(8,128)(2,1)} %param.27, f32[4,32,5120]{2,1,0:T(8,128)} %get-tuple-element.16, f32[5120]{0:T(1024)S(1)} %convert_element_type.73, f32[4,32]{1,0:T(4,128)S(1)} %add_rsqrt_fusion.2), kind=kOutput, calls=%fused_computation.4 | convolution fusion | flops 22818979840 | bytes 189813248 | tf_op jit(solution)/shard_map/sbd,df->sbf/dot_general | solution.py:69
  229.7 99.1 %all-to-all-done.3 = bf16[256,256,128]{2,1,0:T(8,128)(2,1)} async-done(((bf16[256,256,128]{2,1,0:T(8,128)(2,1)}), bf16[256,256,128]{2,1,0:T(8,128)(2,1)}, u32[]{:S(2)}, u32[]{:S(2)}) %all-to-all-start.3) | async-done | bytes 16777248 | tf_op jit(solution)/shard_map/all_to_all | solution.py:113
  328.8 4.9 all-to-all-start.2
  333.7 60.5 %fusion.13.clone.8 = bf16[4,32,17408]{2,1,0:T(8,128)(2,1)} fusion(bf16[5120,17408]{1,0:T(8,128)(2,1)} %param.28, f32[4,32,17408]{2,1,0:T(8,128)} %fusion.4, f32[4,32,5120]{2,1,0:T(8,128)S(1)} %copy-done.3, f32[5120]{0:T(1024)S(1)} %convert_element_type.73, f32[4,32]{1,0:T(4,128)S(1)} %add_rsqrt_fusion.2), kind=kOutput, calls=%fused_computation.11.clone.clone.clone.clone.clone.clone.clone.1 | convolution fusion | flops 22832349184 | bytes 194269696 | tf_op jit(solution)/shard_map/sbd,df->sbf/dot_general | solution.py:70
  394.2 58.1 %fusion.49 = bf16[4,32,5120]{2,1,0:T(8,128)(2,1)} fusion(f32[4,32,5120]{2,1,0:T(8,128)S(1)} %copy-done.3, bf16[17408,5120]{1,0:T(8,128)(2,1)} %param.29, bf16[4,32,17408]{2,1,0:T(8,128)(2,1)} %fusion.13.clone.8), kind=kOutput, calls=%fused_computation.35 | convolution fusion | flops 22818324480 | bytes 186646528 | tf_op jit(solution)/shard_map/sbf,fd->sbd/dot_general | solution.py:72
  452.3 32.7 %shard_map.167 = bf16[32,256,8,128]{3,2,1,0:T(8,128)(2,1)} custom-call(s32[32]{0:T(128)} %copy-done.10, bf16[8,32,256,128]{3,2,1,0:T(8,128)(2,1)} %bitcast.45.blocks_ref, bf16[4,32,8,128]{3,2,1,0:T(8,128)(2,1)} %bitcast.208), custom_call_target="tpu_custom_call" | custom-call | flops 1000000000 | bytes 33554432 | tf_op jit(solution)/shard_map/pallas_call | solution.py:89
  485.0 32.7 %all-to-all-done.2 = bf16[256,256,128]{2,1,0:T(8,128)(2,1)} async-done(((bf16[256,256,128]{2,1,0:T(8,128)(2,1)}), bf16[256,256,128]{2,1,0:T(8,128)(2,1)}, u32[]{:S(2)}, u32[]{:S(2)}) %all-to-all-start.2) | async-done | bytes 16777248 | tf_op jit(solution)/shard_map/all_to_all | solution.py:113
  517.7 32.7 %shard_map.166 = bf16[32,256,8,128]{3,2,1,0:T(8,128)(2,1)} custom-call(s32[32]{0:T(128)} %copy-done.10, bf16[8,32,256,128]{3,2,1,0:T(8,128)(2,1)} %bitcast.44.blocks_ref, bf16[4,32,8,128]{3,2,1,0:T(8,128)(2,1)} %pad_maximum_fusion.1.fresh_ref), custom_call_target="tpu_custom_call" | custom-call | flops 1000000000 | bytes 33554432 | tf_op jit(solution)/shard_map/pallas_call | solution.py:89
  (26 shorter events, 0.3 us)
Async XLA Ops:
  2.7 0.6 copy-start.10
  5.7 6.9 %copy-start.1 = (bf16[4,32,5120]{2,1,0:T(8,128)(2,1)S(1)}, bf16[4,32,5120]{2,1,0:T(8,128)(2,1)}, u32[]{:S(2)}) copy-start(bf16[4,32,5120]{2,1,0:T(8,128)(2,1)} %param.16) | copy-start | bytes 3932164
  5.7 7.9 %copy-start.4 = (bf16[5120,1024]{1,0:T(8,128)(2,1)S(1)}, bf16[5120,1024]{1,0:T(8,128)(2,1)}, u32[]{:S(2)}) copy-start(bf16[5120,1024]{1,0:T(8,128)(2,1)} %param.21) | copy-start | bytes 31457284
  11.8 0.7 copy-start.6
  16.2 18.4 %copy-start.7 = (bf16[4,32,8,64]{3,2,1,0:T(8,128)(2,1)}, bf16[4,32,8,64]{3,2,1,0:T(8,128)(2,1)S(1)}, u32[]{:S(2)}) copy-start(bf16[4,32,8,64]{3,2,1,0:T(8,128)(2,1)S(1)} %get-tuple-element.8) | copy-start | bytes 393220
  34.6 1.5 copy-start.2
  42.6 4.5 copy-start.11
  42.6 28.3 %all-to-all-start = ((bf16[8,28,32,128]{3,2,1,0:T(8,128)(2,1)}), bf16[8,28,32,128]{3,2,1,0:T(8,128)(2,1)S(1)}, u32[]{:S(2)}, u32[]{:S(2)}) async-start(bf16[8,28,32,128]{3,2,1,0:T(8,128)(2,1)} %pad_maximum_fusion), calls=%async_computation | async-start | bytes 3670016 | tf_op jit(solution)/shard_map/all_to_all | solution.py:113
  98.4 6.8 %copy-start = (f32[256,4,5,256]{3,2,1,0:T(8,128)S(1)}, f32[256,4,5,256]{3,2,1,0:T(8,128)}, u32[]{:S(2)}) copy-start(f32[256,4,5,256]{3,2,1,0:T(8,128)} %get-tuple-element.12) | copy-start | bytes 15728644
  116.9 4.0 copy-start.9
  117.0 4.0 copy-start.8
  118.6 20.4 %all-to-all-start.1 = ((bf16[8,4,5,32,128]{4,3,2,1,0:T(8,128)(2,1)}), bf16[8,4,5,32,128]{4,3,2,1,0:T(8,128)(2,1)S(1)}, u32[]{:S(2)}, u32[]{:S(2)}) async-start(bf16[8,4,5,32,128]{4,3,2,1,0:T(8,128)(2,1)} %bitcast.202), calls=%async_computation.1 | async-start | bytes 2621440 | tf_op jit(solution)/shard_map/all_to_all | solution.py:113
  139.0 1.1 copy-start.5
  140.1 188.7 %all-to-all-start.3 = ((bf16[256,256,128]{2,1,0:T(8,128)(2,1)}), bf16[256,256,128]{2,1,0:T(8,128)(2,1)}, u32[]{:S(2)}, u32[]{:S(2)}) async-start(bf16[256,256,128]{2,1,0:T(8,128)(2,1)} %bitcast.193), calls=%async_computation.3 | async-start | bytes 33554432 | tf_op jit(solution)/shard_map/all_to_all | solution.py:113
  328.8 4.9 copy-start.3
  328.8 188.9 %all-to-all-start.2 = ((bf16[256,256,128]{2,1,0:T(8,128)(2,1)}), bf16[256,256,128]{2,1,0:T(8,128)(2,1)}, u32[]{:S(2)}, u32[]{:S(2)}) async-start(bf16[256,256,128]{2,1,0:T(8,128)(2,1)} %bitcast.192), calls=%async_computation.2 | async-start | bytes 33554432 | tf_op jit(solution)/shard_map/all_to_all | solution.py:113

commit v2 on v1

--- a/solution.py
+++ b/solution.py
@@ -1,3 +1,5 @@
+import functools
+
 import jax
 import jax.numpy as jnp
 from jax import lax
@@ -73,34 +75,52 @@
     return (residual.astype(jnp.float32) + down_val).astype(jnp.bfloat16)
 
 
-def merge_kernel(pos_ref, blocks_ref, fresh_ref, out_ref, wide_ref):
-    num_heads = blocks_ref.shape[0]
-    for head_idx in range(num_heads):
-        wide_ref[:, head_idx, :] = blocks_ref[head_idx, 0].astype(jnp.float32)
-    out_ref[0] = wide_ref[...].astype(out_ref.dtype)
-    first_slot = pos_ref[pl.program_id(0)]
+ROW_PAD = 9
+K_CUTS, V_CUTS = (8, 20, 32), (14, 26, 32)
+SWAP_ORDER = (2, 4, 3, 5, 6, 7, 1)
+
+
+def cuts(num_rows, ends):
+    ends = [num_rows * e // 32 for e in ends]
+    return [(lo, hi - lo) for lo, hi in zip([0] + ends[:-1], ends)]
+
+
+def merge_kernel(row_base, meta_ref, *refs):
+    n_dev = (len(refs) - 4) if len(refs) > 11 else (len(refs) - 3)
+    block_refs, fresh_ref = refs[:n_dev], refs[n_dev]
+    out_ref, wide_ref = refs[-2], refs[-1]
+    num_slots = out_ref.shape[1]
+    for rel_idx in range(n_dev):
+        head_idx = meta_ref[rel_idx]
+        wide_ref[pl.ds(head_idx, num_slots, stride=ROW_PAD), :] = block_refs[rel_idx][0].astype(jnp.float32)
+    for slot_idx in range(num_slots):
+        out_ref[0, slot_idx] = wide_ref[slot_idx * ROW_PAD:slot_idx * ROW_PAD + n_dev, :].astype(out_ref.dtype)
+    first_slot = meta_ref[n_dev + row_base + pl.program_id(0)]
     for step_idx in range(fresh_ref.shape[0]):
         out_ref[0, first_slot + step_idx] = fresh_ref[step_idx, 0]
 
 
-def merge_heads(blocks, fresh_rows, start_pos):
-    num_heads, num_rows, num_slots, head_dim = blocks.shape
+def merge_heads(own, blocks, fresh_rows, meta, partial_out, row_base, num_rows):
+    n_dev = len(blocks) + 1
+    chunk_rows, num_slots, head_dim = blocks[0].shape
     n_steps = fresh_rows.shape[0]
+    grid_spec = pltpu.PrefetchScalarGridSpec(
+        num_scalar_prefetch=1,
+        grid=(chunk_rows,),
+        in_specs=[pl.BlockSpec((1, num_slots, head_dim), lambda b, meta: (meta[0] * num_rows + row_base + b, 0, 0))]
+        + [pl.BlockSpec((1, num_slots, head_dim), lambda b, meta: (b, 0, 0))] * (n_dev - 1)
+        + [pl.BlockSpec((n_steps, 1, n_dev, head_dim), lambda b, meta: (0, row_base + b, 0, 0))]
+        + ([] if partial_out is None else [pl.BlockSpec(memory_space=pl.ANY)]),
+        out_specs=pl.BlockSpec((1, num_slots, n_dev, head_dim), lambda b, meta: (row_base + b, 0, 0, 0)),
+        scratch_shapes=[pltpu.VMEM((num_slots * ROW_PAD, head_dim), jnp.float32)],
+    )
     return pl.pallas_call(
-        merge_kernel,
-        out_shape=jax.ShapeDtypeStruct((num_rows, num_slots, num_heads, head_dim), blocks.dtype),
-        grid_spec=pltpu.PrefetchScalarGridSpec(
-            num_scalar_prefetch=1,
-            grid=(num_rows,),
-            in_specs=[
-                pl.BlockSpec((num_heads, 1, num_slots, head_dim), lambda b, pos: (0, b, 0, 0)),
-                pl.BlockSpec((n_steps, 1, num_heads, head_dim), lambda b, pos: (0, b, 0, 0)),
-            ],
-            out_specs=pl.BlockSpec((1, num_slots, num_heads, head_dim), lambda b, pos: (b, 0, 0, 0)),
-            scratch_shapes=[pltpu.VMEM((num_slots, num_heads, head_dim), jnp.float32)],
-        ),
-        cost_estimate=pl.CostEstimate(flops=10**9, bytes_accessed=2 * blocks.size * 2, transcendentals=0),
-    )(start_pos, blocks, fresh_rows)
+        functools.partial(merge_kernel, row_base),
+        out_shape=jax.ShapeDtypeStruct((num_rows, num_slots, n_dev, head_dim), own.dtype),
+        grid_spec=grid_spec,
+        input_output_aliases={} if partial_out is None else {n_dev + 2: 0},
+        cost_estimate=pl.CostEstimate(flops=10**8, bytes_accessed=4 * n_dev * blocks[0].size, transcendentals=0),
+    )(meta, own, *blocks, fresh_rows, *(() if partial_out is None else (partial_out,)))
 
 
 def solution(mesh):
@@ -109,15 +129,21 @@
     cache_in = P('dp', None, 'x', None)
     cache_out = P(('dp', 'x'), None, None, None)
 
-    def swap(arr):
-        return lax.all_to_all(arr, 'x', 0, 0, tiled=True)
-
     def local_run(start_pos, hidden_in, k_heads, v_heads, attn_norm, w_q, w_k, w_v, q_norm, k_norm, w_o, mlp_norm, w_gate, w_up, w_down):
         n_steps, num_rows, _ = hidden_in.shape
-        all_rows, num_slots, _, head_dim = k_heads.shape
-        my_pos = lax.dynamic_slice_in_dim(start_pos, lax.axis_index('x') * num_rows, num_rows)
+        all_rows, _, _, head_dim = k_heads.shape
+        me = lax.axis_index('x')
+        my_pos = lax.dynamic_slice_in_dim(start_pos, me * num_rows, num_rows)
         k_own, v_own = k_heads[:, :, 0], v_heads[:, :, 0]
-        k_got = swap(k_own).reshape(n_dev, num_rows, num_slots, head_dim)
+
+        def swap(arr, rel_idx):
+            return lax.ppermute(arr, 'x', [(d, d ^ rel_idx) for d in range(n_dev)])
+
+        def swap_cache(own, row_base, chunk_rows):
+            return [swap(lax.dynamic_slice_in_dim(own, jnp.bitwise_xor(me, rel_idx) * num_rows + row_base, chunk_rows), rel_idx) for rel_idx in SWAP_ORDER]
+
+        cuts_k, cuts_v = cuts(num_rows, K_CUTS), cuts(num_rows, V_CUTS)
+        k_got = [swap_cache(k_own, *c) for c in cuts_k]
         positions = my_pos[None, :] + jnp.arange(n_steps)[:, None]
         queries, keys_new, values_new = project(hidden_in, positions, attn_norm, w_q, w_k, w_v, q_norm, k_norm)
         group = queries.shape[2] // n_dev
@@ -125,19 +151,33 @@
         k_send = keys_new.transpose(2, 0, 1, 3)
         v_send = values_new.transpose(2, 0, 1, 3)
         sent = jnp.concatenate([q_send, k_send, v_send], axis=1)
-        got = swap(sent)
-        got = got.transpose(1, 0, 2, 3).reshape(n_steps * (group + 2), all_rows, head_dim)
+        got = jnp.zeros((n_steps * (group + 2), n_dev, num_rows, head_dim), sent.dtype)
+        for rel_idx in range(n_dev):
+            peer = jnp.bitwise_xor(me, rel_idx)
+            part = lax.dynamic_index_in_dim(sent, peer, 0, keepdims=False)
+            part = swap(part, rel_idx) if rel_idx else part
+            got = lax.dynamic_update_slice_in_dim(got, part[:, None], peer, 1)
+        got = got.reshape(n_steps * (group + 2), all_rows, head_dim)
         q_got = got[:n_steps * group].reshape(n_steps, group, all_rows, head_dim).transpose(0, 2, 1, 3)
         kn_got = got[n_steps * group:n_steps * (group + 1), :, None]
         vn_got = got[n_steps * (group + 1):, :, None]
         mixed = attend(q_got, k_heads, v_heads, kn_got, vn_got, start_pos)
         mixed = mixed.reshape(n_steps, n_dev, num_rows, group, head_dim).transpose(1, 0, 3, 2, 4)
-        v_got = swap(v_own).reshape(n_dev, num_rows, num_slots, head_dim)
-        back = swap(mixed)
+        v_got = [swap_cache(v_own, *c) for c in cuts_v]
+        back = jnp.zeros_like(mixed)
+        for rel_idx in range(n_dev):
+            peer = jnp.bitwise_xor(me, rel_idx)
+            part = lax.dynamic_index_in_dim(mixed, peer, 0)
+            part = swap(part, rel_idx) if rel_idx else part
+            back = lax.dynamic_update_slice_in_dim(back, part, peer, 0)
         attended = back.transpose(1, 3, 0, 2, 4).reshape(n_steps, num_rows, n_dev * group, head_dim)
         out_hidden = finish(hidden_in, attended, w_o, mlp_norm, w_gate, w_up, w_down)
-        k_out = merge_heads(k_got, keys_new, my_pos)
-        v_out = merge_heads(v_got, values_new, my_pos)
+        meta = jnp.concatenate([jnp.bitwise_xor(me, jnp.array((0,) + SWAP_ORDER)), my_pos]).astype(jnp.int32)
+        k_out = v_out = None
+        for (row_base, chunk_rows), k_blocks in zip(cuts_k, k_got):
+            k_out = merge_heads(k_own, k_blocks, keys_new, meta, k_out, row_base, num_rows)
+        for (row_base, chunk_rows), v_blocks in zip(cuts_v, v_got):
+            v_out = merge_heads(v_own, v_blocks, values_new, meta, v_out, row_base, num_rows)
         return out_hidden, k_out, v_out
 
     return jax.shard_map(local_run, mesh=mesh, in_specs=(P('dp'), row_spec, cache_in, cache_in) + (P(),) * 11, out_specs=(row_spec, cache_out, cache_out), check_vma=False)

time: 560 us -> 645 us (1.15)
  local copies, waits for them, and re-layouts: 13 us -> 49.7 us
  starting transfers between devices: 16.5 us -> 52.3 us
  waiting for transfers between devices: 173 us -> 197 us
  Pallas kernels: 65.4 us -> 55.7 us
    ppermute x0 -> x56, waiting for transfers between devices: none -> 197 us  [swap(): return lax.ppermute(arr, 'x', [(d, d ^ rel_idx) for d in range(n_dev)])]
    all_to_all x4 -> x0, waiting for transfers between devices: 173 us -> none  [swap(): return lax.all_to_all(arr, 'x', 0, 0, tiled=True)]
    ppermute x0 -> x56, starting transfers between devices: none -> 52.3 us  [swap(): return lax.ppermute(arr, 'x', [(d, d ^ rel_idx) for d in range(n_dev)])]
    dynamic_slice x1 -> x6, local copies, waits for them, and re-layouts: 0.75 us -> 25.4 us  [the longest x5 25.3 us: swap_cache(): lax.dynamic_slice_in_dim(own, jnp.bitwise_xor(me, rel_idx) * num_rows + r...]
    all_to_all x4 -> x0, starting transfers between devices: 16.5 us -> none  [swap(): return lax.all_to_all(arr, 'x', 0, 0, tiled=True)]
    pallas_call x2 -> x6, Pallas kernels: 65.4 us -> 55.7 us  [merge_heads(): pl.pallas_call(functools.partial(merge_kernel, row_base), out_shape=jax.S...]
  transfers between devices with their start and end apart: 4 -> 56, of which waited for: 4 -> 14; matrix products, arithmetic and copies ran while one was open for 37% -> 50% of each run, Pallas kernels for 6% -> 8%
where the time goes in v2:
time: 645 us; the launch traced here: 636 us
  matrix products  262 us (41%)
  waiting for transfers between devices  197 us (31%)
  Pallas kernels  55.7 us (9%)
  starting transfers between devices  52.3 us (8%)
  local copies, waits for them, and re-layouts  49.7 us (8%)
  other arithmetic  17.6 us (3%)
    ppermute x56, waiting for transfers between devices, swap(): return lax.ppermute(arr, 'x', [(d, d ^ rel_idx) for d in range(n_dev)])  197 us
    dot_general x1, matrix products, finish(): jnp.einsum('sbd,df->sbf', normed, w_gate, preferred_element_type=jnp.floa...  64.3 us
    dot_general x1, matrix products, finish(): jnp.einsum('sbd,df->sbf', normed, w_up, preferred_element_type=jnp.float32)  60.5 us
    dot_general x1, matrix products, finish(): jnp.einsum('sbf,fd->sbd', activated, w_down, preferred_element_type=jnp.f...  58.1 us
    pallas_call x6, Pallas kernels, merge_heads(): pl.pallas_call(functools.partial(merge_kernel, row_base), out_shape=jax.S...  55.7 us
    ppermute x56, starting transfers between devices, swap(): return lax.ppermute(arr, 'x', [(d, d ^ rel_idx) for d in range(n_dev)])  52.3 us
    dynamic_slice x5, local copies, waits for them, and re-layouts, swap_cache(): lax.dynamic_slice_in_dim(own, jnp.bitwise_xor(me, rel_idx) * num_rows + r...  25.3 us
    dot_general x1, matrix products, finish(): jnp.einsum('sbe,ed->sbd', flat_attn, w_o, preferred_element_type=jnp.floa...  20.8 us
  transfers between devices with their start and end apart: 56, of which 14 were waited for; matrix products, arithmetic and copies ran while one was open for 50% of the time, Pallas kernels for 8%

profile of v2, /device:TPU:0, one launch (start us, length us, event | category | flops | bytes accessed | tf_op | source)
XLA Modules:
  0.0 635.5 jit_solution(11012104140682625292)
XLA Ops:
  0.7 3.4 dynamic-slice_bitcast_fusion.35
  4.1 3.3 collective-permute-start.35
  7.4 1.5 collective-permute-start.36
  9.4 5.7 fusion.24
  16.4 1.7 fusion.82
  19.9 18.1 %fusion.8 = f32[4,32,5120]{2,1,0:T(8,128)S(1)} fusion(bf16[5120,5120]{1,0:T(8,128)(2,1)} %param.21, bf16[4,32,5120]{2,1,0:T(8,128)(2,1)S(1)} %copy-done.1, f32[5120]{0:T(1024)S(1)} %convert_element_type.61, f32[4,32]{1,0:T(4,128)S(1)} %add_rsqrt_fusion.3), kind=kOutput, calls=%fused_computation.8 | convolution fusion | flops 6713507840 | bytes 56381952 | tf_op jit(solution)/shard_map/sbd,de->sbe/dot_general | solution.py:36
  40.4 2.3 fusion.66
  44.4 1.4 copy.50
  46.5 1.6 pad_maximum_fusion
  48.2 1.2 dynamic-slice_bitcast_fusion.42
  49.9 1.3 collective-permute-start.2
  53.3 4.8 collective-permute-done.1
  59.1 3.0 collective-permute-done.2
  63.6 2.3 collective-permute-start.6
  66.0 5.6 collective-permute-done.5
  71.5 3.9 collective-permute-done.6
  76.8 9.7 %fusion.98 = (f32[256,5,4]{1,2,0:T(4,128)S(1)}, f32[256,1,5,4,4]{2,4,3,0,1:T(4,128)S(1)}) fusion(bf16[4,256,128,1]{2,0,3,1:T(4,128)(2,1)S(1)} %bitcast.352, bf16[4,5,256,128]{3,2,1,0:T(8,128)(2,1)S(1)} %bitcast.331, pred[4,4]{1,0:T(4,128)(4,1)S(1)} %iota_compare_fusion.1), kind=kOutput, calls=%fused_computation.182 | convolution fusion | flops 5299200 | bytes 1675280 | tf_op jit(solution)/shard_map/sbkgd,jbkd->bkgsj/dot_general | solution.py:52
  86.5 12.1 %fusion.34 = (f32[256,5,4]{1,2,0:T(4,128)S(1)}, f32[256,4,5,256]{3,2,1,0:T(8,128)}) fusion(pred[256,256]{1,0:T(8,128)(4,1)S(1)} %iota_compare_fusion, bf16[256,256,1,128]{3,1,2,0:T(8,128)(2,1)} %param.18, bf16[4,5,256,128]{3,2,1,0:T(8,128)(2,1)S(1)} %bitcast.332), kind=kOutput, calls=%fused_computation.30 | convolution fusion | flops 339471360 | bytes 23416832 | tf_op jit(solution)/shard_map/sbkgd,btkd->bkgst/dot_general | solution.py:49
  98.7 6.8 %fusion.32 = f32[256,5,4]{1,2,0:T(4,128)S(1)} fusion(f32[256,4,5,256]{3,2,1,0:T(8,128)} %get-tuple-element.69, f32[256,5,4]{1,2,0:T(4,128)S(1)} %max.8, pred[256,256]{1,0:T(8,128)(4,1)S(1)} %iota_compare_fusion), kind=kLoop, calls=%fused_computation.28 | loop fusion | flops 5237760 | bytes 5349376 | tf_op jit(solution)/shard_map/reduce_sum | solution.py:58
  105.5 8.0 %fusion.18 = f32[256,5,4,128]{3,1,2,0:T(8,128)S(1)} fusion(bf16[256,256,1,128]{3,1,2,0:T(8,128)(2,1)} %param.19, f32[256,4,5,256]{3,2,1,0:T(8,128)S(1)} %copy-done, f32[256,5,4]{1,2,0:T(4,128)S(1)} %max.8, pred[256,256]{1,0:T(8,128)(4,1)S(1)} %iota_compare_fusion), kind=kOutput, calls=%fused_computation.12 | convolution fusion | flops 340787200 | bytes 24727552 | tf_op jit(solution)/shard_map/bkgst,btkd->sbkgd/dot_general | solution.py:59
  113.5 1.9 fusion.74
  115.8 2.8 fusion.57
  118.6 1.2 constant_dynamic-slice_fusion
  124.7 1.4 collective-permute-start.11
  126.4 3.7 collective-permute-done.8
  130.8 3.7 dynamic-slice_bitcast_fusion.28
  136.9 12.5 %collective-permute-done.11 = bf16[1,4,5,32,128]{4,2,0,3,1:T(8,128)(2,1)S(1)} collective-permute-done((bf16[1,4,5,32,128]{4,2,0,3,1:T(8,128)(2,1)S(1)}, bf16[1,4,5,32,128]{4,2,0,3,1:T(8,128)(2,1)S(1)}, u32[]{:S(2)}, u32[]{:S(2)}) %collective-permute-start.11) | collective-permute-done | bytes 163872 | tf_op jit(solution)/shard_map/ppermute | solution.py:140
  151.2 2.2 collective-permute-start.32
  153.4 7.6 %dynamic-slice_bitcast_fusion.14 = (bf16[12,256,128]{2,1,0:T(8,128)(2,1)}, bf16[12,256,128]{2,1,0:T(8,128)(2,1)}, bf16[12,256,128]{2,1,0:T(8,128)(2,1)}, bf16[12...) fusion(bf16[256,256,1,128]{3,1,2,0:T(8,128)(2,1)} %param.18, ...), kind=kLoop, calls=%fused_computation.90 | loop fusion | bytes 22020152 | tf_op jit(solution)/shard_map/dynamic_slice | solution.py:143
  162.4 5.6 collective-permute-done.30.refs_3_
  167.9 1.8 collective-permute-start.23
  169.7 13.4 %collective-permute-done.31.refs_4_ = bf16[8,256,128]{2,1,0:T(8,128)(2,1)S(1)} collective-permute-done((bf16[8,256,128]{2,1,0:T(8,128)(2,1)}, bf16[8,256,128]{2,1,0:T(8,128)(2,1)S(1)}, u32[]{:S(2)}, u32[]{:S(2)}) %collective-permute-start.31) | collective-permute-done | bytes 524320 | tf_op jit(solution)/shard_map/ppermute | solution.py:140
  184.1 40.0 %collective-permute-done.33.refs_6_ = bf16[8,256,128]{2,1,0:T(8,128)(2,1)S(1)} collective-permute-done((bf16[8,256,128]{2,1,0:T(8,128)(2,1)S(1)}, bf16[8,256,128]{2,1,0:T(8,128)(2,1)S(1)}, u32[]{:S(2)}, u32[]{:S(2)}) %collective-permute-start.33) | collective-permute-done | bytes 524320 | tf_op jit(solution)/shard_map/ppermute | solution.py:140
  224.1 1.7 collective-permute-start.24
  226.1 1.9 collective-permute-start.26
  230.4 5.0 dynamic-slice_bitcast_fusion.7
  235.3 5.7 dynamic-slice_bitcast_fusion
  241.7 35.5 %collective-permute-done.24.refs_4_ = bf16[12,256,128]{2,1,0:T(8,128)(2,1)} collective-permute-done((bf16[12,256,128]{2,1,0:T(8,128)(2,1)}, bf16[12,256,128]{2,1,0:T(8,128)(2,1)}, u32[]{:S(2)}, u32[]{:S(2)}) %collective-permute-start.24) | collective-permute-done | bytes 786464 | tf_op jit(solution)/shard_map/ppermute | solution.py:140
  277.2 1.5 collective-permute-start.15
  279.7 2.2 collective-permute-start.18
  285.1 2.3 reshape_reshape.7
  287.4 10.5 %collective-permute-done.15.refs_2_ = bf16[12,256,128]{2,1,0:T(8,128)(2,1)} collective-permute-done((bf16[12,256,128]{2,1,0:T(8,128)(2,1)}, bf16[12,256,128]{2,1,0:T(8,128)(2,1)}, u32[]{:S(2)}, u32[]{:S(2)}) %collective-permute-start.15) | collective-permute-done | bytes 786464 | tf_op jit(solution)/shard_map/ppermute | solution.py:140
  298.1 1.1 collective-permute-start.42
  299.2 49.1 %collective-permute-done.17.refs_4_ = bf16[12,256,128]{2,1,0:T(8,128)(2,1)} collective-permute-done((bf16[12,256,128]{2,1,0:T(8,128)(2,1)}, bf16[12,256,128]{2,1,0:T(8,128)(2,1)}, u32[]{:S(2)}, u32[]{:S(2)}) %collective-permute-start.17) | collective-permute-done | bytes 786464 | tf_op jit(solution)/shard_map/ppermute | solution.py:140
  348.3 1.5 collective-permute-start.43
  350.4 20.8 %multiply_reduce_fusion = (f32[4,32]{1,0:T(4,128)S(1)}, f32[4,32,5120]{2,1,0:T(8,128)}) fusion(bf16[4,32,5120]{2,1,0:T(8,128)(2,1)} %reshape_reshape.7, bf16[5120,5120]{1,0:T(8,128)(2,1)} %param.26, bf16[4,32,5120]{2,1,0:T(8,128)(2,1)S(1)} %copy-done.1), kind=kOutput, calls=%fused_computation.55 | convolution fusion | flops 6714818560 | bytes 57672192 | tf_op jit(solution)/shard_map/sbe,ed->sbd/dot_general | solution.py:68
  371.2 1.8 collective-permute-start.49
  372.9 1.5 collective-permute-start.50
  374.7 1.3 collective-permute-start.47
  376.0 9.0 %collective-permute-done.45.refs_4_ = bf16[12,256,128]{2,1,0:T(8,128)(2,1)S(1)} collective-permute-done((bf16[12,256,128]{2,1,0:T(8,128)(2,1)}, bf16[12,256,128]{2,1,0:T(8,128)(2,1)S(1)}, u32[]{:S(2)}, u32[]{:S(2)}) %collective-permute-start.45) | collective-permute-done | bytes 786464 | tf_op jit(solution)/shard_map/ppermute | solution.py:140
  386.1 64.3 %fusion.4 = f32[4,32,17408]{2,1,0:T(8,128)} fusion(bf16[5120,17408]{1,0:T(8,128)(2,1)} %param.28, f32[4,32,5120]{2,1,0:T(8,128)} %get-tuple-element.73, f32[5120]{0:T(1024)S(1)} %convert_element_type.73, f32[4,32]{1,0:T(4,128)S(1)} %add_rsqrt_fusion.2), kind=kOutput, calls=%fused_computation.4 | convolution fusion | flops 22818979840 | bytes 189813248 | tf_op jit(solution)/shard_map/sbd,df->sbf/dot_general | solution.py:71
  451.1 1.2 collective-permute-start.52
  452.3 1.5 collective-permute-start.53
  453.8 1.4 collective-permute-start.54
  455.4 60.5 %fusion.13.clone.8 = bf16[4,32,17408]{2,1,0:T(8,128)(2,1)} fusion(bf16[5120,17408]{1,0:T(8,128)(2,1)} %param.29, f32[4,32,17408]{2,1,0:T(8,128)} %fusion.4, f32[4,32,5120]{2,1,0:T(8,128)S(1)} %copy-done.3, f32[5120]{0:T(1024)S(1)} %convert_element_type.73, f32[4,32]{1,0:T(4,128)S(1)} %add_rsqrt_fusion.2), kind=kOutput, calls=%fused_computation.11.clone.clone.clone.clone.clone.clone.clone.1 | convolution fusion | flops 22832349184 | bytes 194269696 | tf_op jit(solution)/shard_map/sbd,df->sbf/dot_general | solution.py:72
  515.8 1.4 collective-permute-start.37
  517.6 1.5 collective-permute-start.39
  520.6 58.1 %fusion.49 = bf16[4,32,5120]{2,1,0:T(8,128)(2,1)} fusion(f32[4,32,5120]{2,1,0:T(8,128)S(1)} %copy-done.3, bf16[17408,5120]{1,0:T(8,128)(2,1)} %param.30, bf16[4,32,17408]{2,1,0:T(8,128)(2,1)} %fusion.13.clone.8), kind=kOutput, calls=%fused_computation.35 | convolution fusion | flops 22818324480 | bytes 186646528 | tf_op jit(solution)/shard_map/sbf,fd->sbd/dot_general | solution.py:74
  578.7 7.5 %shard_map.175.refs_9_ = bf16[32,256,8,128]{3,2,1,0:T(8,128)(2,1)} custom-call(s32[40]{0:T(128)} %pad_add_fusion.meta_ref, bf16[256,256,128]{2,1,0:T(8,128)(2,1)} %bitcast.324, bf16[8,256,128]{2,1,0:T(8,128)(2,1)} %copy-done.16, bf16[8,256,128]{2,1,0:T(8,128)(2,1)} %copy-done.17, bf16[8,256,128]{2,1,0:T(8,128)(2,1)} %copy-done.18, ...), custom_call_target="tpu_custom_call" | custom-call | flops 100000000 | bytes 8388608 | tf_op jit(solution)/shard_map/pallas_call | solution.py:117
  586.2 10.2 %shard_map.176.refs_9_ = bf16[32,256,8,128]{3,2,1,0:T(8,128)(2,1)} custom-call(s32[40]{0:T(128)} %pad_add_fusion.meta_ref, bf16[256,256,128]{2,1,0:T(8,128)(2,1)} %bitcast.325, bf16[12,256,128]{2,1,0:T(8,128)(2,1)} %copy-done.8, bf16[12,256,128]{2,1,0:T(8,128)(2,1)} %copy-done.9, bf16[12,256,128]{2,1,0:T(8,128)(2,1)} %copy-done.10, ...), custom_call_target="tpu_custom_call", output_to_operand_aliasing={{}: (10, {})} | custom-call | flops 100000000 | bytes 12582912 | tf_op jit(solution)/shard_map/pallas_call | solution.py:117
  596.4 10.2 %shard_map.177 = bf16[32,256,8,128]{3,2,1,0:T(8,128)(2,1)} custom-call(s32[40]{0:T(128)} %pad_add_fusion.meta_ref, bf16[256,256,128]{2,1,0:T(8,128)(2,1)} %bitcast.326, bf16[12,256,128]{2,1,0:T(8,128)(2,1)} %collective-permute-done.14.refs_1_, bf16[12,256,128]{2,1,0:T(8,128)(2,1)} %collective-permute-done.15.refs_2_, ...), custom_call_target="tpu_custom_call", output_to_operand_aliasing={{}: (10, {})} | custom-call | flops 100000000 | bytes 12582912 | tf_op jit(solution)/shard_map/pallas_call | solution.py:117
  606.6 11.5 %shard_map.178.refs_9_ = bf16[32,256,8,128]{3,2,1,0:T(8,128)(2,1)} custom-call(s32[40]{0:T(128)} %pad_add_fusion.meta_ref, bf16[256,256,128]{2,1,0:T(8,128)(2,1)} %bitcast.327, bf16[14,256,128]{2,1,0:T(8,128)(2,1)} %collective-permute-done.49.refs_1_, bf16[14,256,128]{2,1,0:T(8,128)(2,1)} %collective-permute-done.50.refs_2_, ...), custom_call_target="tpu_custom_call" | custom-call | flops 100000000 | bytes 14680064 | tf_op jit(solution)/shard_map/pallas_call | solution.py:117
  618.1 10.2 %shard_map.179.refs_9_ = bf16[32,256,8,128]{3,2,1,0:T(8,128)(2,1)} custom-call(s32[40]{0:T(128)} %pad_add_fusion.meta_ref, bf16[256,256,128]{2,1,0:T(8,128)(2,1)} %bitcast.328, bf16[12,256,128]{2,1,0:T(8,128)(2,1)} %copy-done.11, bf16[12,256,128]{2,1,0:T(8,128)(2,1)} %copy-done.13, ...), custom_call_target="tpu_custom_call", output_to_operand_aliasing={{}: (10, {})} | custom-call | flops 100000000 | bytes 12582912 | tf_op jit(solution)/shard_map/pallas_call | solution.py:117
  629.2 6.2 shard_map.180
  (230 shorter events, 40.3 us)
Async XLA Ops:
  4.1 120.1 %collective-permute-start.35 = (bf16[6,256,128]{2,1,0:T(8,128)(2,1)}, bf16[6,256,128]{2,1,0:T(8,128)(2,1)}, u32[]{:S(2)}, u32[]{:S(2)}) collective-permute-start(bf16[6,256,128]{2,1,0:T(8,128)(2,1)} %get-tuple-element.23), channel_id=1, source_target_pairs={{0,2},{1,3},{2,0},{3,1},{4,6},{5,7},{6,4},{7,5}} | collective-permute-start | bytes 1179656 | tf_op jit(solution)/shard_map/ppermute | solution.py:140
  7.4 117.3 %collective-permute-start.36 = (bf16[6,256,128]{2,1,0:T(8,128)(2,1)}, bf16[6,256,128]{2,1,0:T(8,128)(2,1)}, u32[]{:S(2)}, u32[]{:S(2)}) collective-permute-start(bf16[6,256,128]{2,1,0:T(8,128)(2,1)} %get-tuple-element.22), channel_id=1, source_target_pairs={{0,4},{1,5},{2,6},{3,7},{4,0},{5,1},{6,2},{7,3}} | collective-permute-start | bytes 1179656 | tf_op jit(solution)/shard_map/ppermute | solution.py:140
  49.4 2.4 collective-permute-start
  49.4 8.8 %collective-permute-start.1 = (bf16[28,32,128]{2,1,0:T(8,128)(2,1)}, bf16[28,32,128]{2,1,0:T(8,128)(2,1)}, u32[]{:S(2)}, u32[]{:S(2)}) collective-permute-start(bf16[28,32,128]{2,1,0:T(8,128)(2,1)} %get-tuple-element.62), channel_id=1, source_target_pairs={{0,2},{1,3},{2,0},{3,1},{4,6},{5,7},{6,4},{7,5}} | collective-permute-start | bytes 688136 | tf_op jit(solution)/shard_map/ppermute | solution.py:140
  49.9 12.2 %collective-permute-start.2 = (bf16[28,32,128]{2,1,0:T(8,128)(2,1)}, bf16[28,32,128]{2,1,0:T(8,128)(2,1)}, u32[]{:S(2)}, u32[]{:S(2)}) collective-permute-start(bf16[28,32,128]{2,1,0:T(8,128)(2,1)} %get-tuple-element.61), channel_id=1, source_target_pairs={{0,3},{1,2},{2,1},{3,0},{4,7},{5,6},{6,5},{7,4}} | collective-permute-start | bytes 688136 | tf_op jit(solution)/shard_map/ppermute | solution.py:140
  51.8 11.7 %collective-permute-start.3 = (bf16[28,32,128]{2,1,0:T(8,128)(2,1)}, bf16[28,32,128]{2,1,0:T(8,128)(2,1)S(1)}, u32[]{:S(2)}, u32[]{:S(2)}) collective-permute-start(bf16[28,32,128]{2,1,0:T(8,128)(2,1)} %get-tuple-element.60), channel_id=1, source_target_pairs={{0,4},{1,5},{2,6},{3,7},{4,0},{5,1},{6,2},{7,3}} | collective-permute-start | bytes 688136 | tf_op jit(solution)/shard_map/ppermute | solution.py:140
  58.1 7.8 %collective-permute-start.4 = (bf16[28,32,128]{2,1,0:T(8,128)(2,1)S(1)}, bf16[28,32,128]{2,1,0:T(8,128)(2,1)S(1)}, u32[]{:S(2)}, u32[]{:S(2)}) collective-permute-start(bf16[28,32,128]{2,1,0:T(8,128)(2,1)S(1)} %copy-done.37), channel_id=1, source_target_pairs={{0,5},{1,4},{2,7},{3,6},{4,1},{5,0},{6,3},{7,2}} | collective-permute-start | bytes 688136 | tf_op jit(solution)/shard_map/ppermute | solution.py:140
  62.1 9.4 %collective-permute-start.5 = (bf16[28,32,128]{2,1,0:T(8,128)(2,1)S(1)}, bf16[28,32,128]{2,1,0:T(8,128)(2,1)S(1)}, u32[]{:S(2)}, u32[]{:S(2)}) collective-permute-start(bf16[28,32,128]{2,1,0:T(8,128)(2,1)S(1)} %copy-done.36), channel_id=1, source_target_pairs={{0,6},{1,7},{2,4},{3,5},{4,2},{5,3},{6,0},{7,1}} | collective-permute-start | bytes 688136 | tf_op jit(solution)/shard_map/ppermute | solution.py:140
  63.6 11.9 %collective-permute-start.6 = (bf16[28,32,128]{2,1,0:T(8,128)(2,1)S(1)}, bf16[28,32,128]{2,1,0:T(8,128)(2,1)S(1)}, u32[]{:S(2)}, u32[]{:S(2)}) collective-permute-start(bf16[28,32,128]{2,1,0:T(8,128)(2,1)S(1)} %get-tuple-element.57), channel_id=1, source_target_pairs={{0,7},{1,6},{2,5},{3,4},{4,3},{5,2},{6,1},{7,0}} | collective-permute-start | bytes 688136 | tf_op jit(solution)/shard_map/ppermute | solution.py:140
  120.5 5.6 collective-permute-start.7
  120.9 9.2 %collective-permute-start.8 = (bf16[1,4,5,32,128]{4,2,0,3,1:T(8,128)(2,1)S(1)}, bf16[1,4,5,32,128]{4,2,0,3,1:T(8,128)(2,1)S(1)}, u32[]{:S(2)}, u32[]{:S(2)}) collective-permute-start(bf16[1,4,5,32,128]{4,2,0,3,1:T(8,128)(2,1)S(1)} %bitcast.347), channel_id=1, source_target_pairs={{0,2},{1,3},{2,0},{3,1},{4,6},{5,7},{6,4},{7,5}} | collective-permute-start | bytes 491528 | tf_op jit(solution)/shard_map/ppermute | solution.py:140
  121.5 13.0 %collective-permute-start.9 = (bf16[1,4,5,32,128]{4,2,0,3,1:T(8,128)(2,1)S(1)}, bf16[1,4,5,32,128]{4,2,0,3,1:T(8,128)(2,1)S(1)}, u32[]{:S(2)}, u32[]{:S(2)}) collective-permute-start(bf16[1,4,5,32,128]{4,2,0,3,1:T(8,128)(2,1)S(1)} %bitcast.350), channel_id=1, source_target_pairs={{0,3},{1,2},{2,1},{3,0},{4,7},{5,6},{6,5},{7,4}} | collective-permute-start | bytes 491528 | tf_op jit(solution)/shard_map/ppermute | solution.py:140
  124.2 11.1 %collective-permute-start.10 = (bf16[1,4,5,32,128]{4,2,0,3,1:T(8,128)(2,1)S(1)}, bf16[1,4,5,32,128]{4,2,0,3,1:T(8,128)(2,1)S(1)}, u32[]{:S(2)}, u32[]{:S(2)}) collective-permute-start(bf16[1,4,5,32,128]{4,2,0,3,1:T(8,128)(2,1)S(1)} %bitcast.349), channel_id=1, source_target_pairs={{0,4},{1,5},{2,6},{3,7},{4,0},{5,1},{6,2},{7,3}} | collective-permute-start | bytes 491528 | tf_op jit(solution)/shard_map/ppermute | solution.py:140
  124.7 24.8 %collective-permute-start.11 = (bf16[1,4,5,32,128]{4,2,0,3,1:T(8,128)(2,1)S(1)}, bf16[1,4,5,32,128]{4,2,0,3,1:T(8,128)(2,1)S(1)}, u32[]{:S(2)}, u32[]{:S(2)}) collective-permute-start(bf16[1,4,5,32,128]{4,2,0,3,1:T(8,128)(2,1)S(1)} %bitcast.348), channel_id=1, source_target_pairs={{0,5},{1,4},{2,7},{3,6},{4,1},{5,0},{6,3},{7,2}} | collective-permute-start | bytes 491528 | tf_op jit(solution)/shard_map/ppermute | solution.py:140
  126.1 25.1 %collective-permute-start.12 = (bf16[1,4,5,32,128]{4,2,0,3,1:T(8,128)(2,1)}, bf16[1,4,5,32,128]{4,2,0,3,1:T(8,128)(2,1)}, u32[]{:S(2)}, u32[]{:S(2)}) collective-permute-start(bf16[1,4,5,32,128]{4,2,0,3,1:T(8,128)(2,1)} %bitcast.314), channel_id=1, source_target_pairs={{0,6},{1,7},{2,4},{3,5},{4,2},{5,3},{6,0},{7,1}} | collective-permute-start | bytes 491528 | tf_op jit(solution)/shard_map/ppermute | solution.py:140
  130.8 20.4 %collective-permute-start.13 = (bf16[1,4,5,32,128]{4,2,0,3,1:T(8,128)(2,1)}, bf16[1,4,5,32,128]{4,2,0,3,1:T(8,128)(2,1)}, u32[]{:S(2)}, u32[]{:S(2)}) collective-permute-start(bf16[1,4,5,32,128]{4,2,0,3,1:T(8,128)(2,1)} %bitcast.313), channel_id=1, source_target_pairs={{0,7},{1,6},{2,5},{3,4},{4,3},{5,2},{6,1},{7,0}} | collective-permute-start | bytes 491528 | tf_op jit(solution)/shard_map/ppermute | solution.py:140
  134.5 26.5 %collective-permute-start.28 = (bf16[8,256,128]{2,1,0:T(8,128)(2,1)}, bf16[8,256,128]{2,1,0:T(8,128)(2,1)S(1)}, u32[]{:S(2)}, u32[]{:S(2)}) collective-permute-start(bf16[8,256,128]{2,1,0:T(8,128)(2,1)} %get-tuple-element.29), channel_id=1, source_target_pairs={{0,2},{1,3},{2,0},{3,1},{4,6},{5,7},{6,4},{7,5}} | collective-permute-start | bytes 1572872 | tf_op jit(solution)/shard_map/ppermute | solution.py:140
  136.0 25.8 %collective-permute-start.29 = (bf16[8,256,128]{2,1,0:T(8,128)(2,1)}, bf16[8,256,128]{2,1,0:T(8,128)(2,1)S(1)}, u32[]{:S(2)}, u32[]{:S(2)}) collective-permute-start(bf16[8,256,128]{2,1,0:T(8,128)(2,1)} %get-tuple-element.28), channel_id=1, source_target_pairs={{0,4},{1,5},{2,6},{3,7},{4,0},{5,1},{6,2},{7,3}} | collective-permute-start | bytes 1572872 | tf_op jit(solution)/shard_map/ppermute | solution.py:140
  150.2 17.8 %collective-permute-start.30 = (bf16[8,256,128]{2,1,0:T(8,128)(2,1)}, bf16[8,256,128]{2,1,0:T(8,128)(2,1)S(1)}, u32[]{:S(2)}, u32[]{:S(2)}) collective-permute-start(bf16[8,256,128]{2,1,0:T(8,128)(2,1)} %get-tuple-element.27), channel_id=1, source_target_pairs={{0,3},{1,2},{2,1},{3,0},{4,7},{5,6},{6,5},{7,4}} | collective-permute-start | bytes 1572872 | tf_op jit(solution)/shard_map/ppermute | solution.py:140
  151.2 32.0 %collective-permute-start.31 = (bf16[8,256,128]{2,1,0:T(8,128)(2,1)}, bf16[8,256,128]{2,1,0:T(8,128)(2,1)S(1)}, u32[]{:S(2)}, u32[]{:S(2)}) collective-permute-start(bf16[8,256,128]{2,1,0:T(8,128)(2,1)} %get-tuple-element.26), channel_id=1, source_target_pairs={{0,5},{1,4},{2,7},{3,6},{4,1},{5,0},{6,3},{7,2}} | collective-permute-start | bytes 1572872 | tf_op jit(solution)/shard_map/ppermute | solution.py:140
  151.2 79.1 %copy-start.39 = (bf16[5120]{0:T(1024)(128)(2,1)S(1)}, bf16[5120]{0:T(1024)(128)(2,1)}, u32[]{:S(2)}) copy-start(bf16[5120]{0:T(1024)(128)(2,1)} %param.27) | copy-start | bytes 30724
  151.2 32.8 %collective-permute-start.32 = (bf16[8,256,128]{2,1,0:T(8,128)(2,1)}, bf16[8,256,128]{2,1,0:T(8,128)(2,1)S(1)}, u32[]{:S(2)}, u32[]{:S(2)}) collective-permute-start(bf16[8,256,128]{2,1,0:T(8,128)(2,1)} %get-tuple-element.25), channel_id=1, source_target_pairs={{0,6},{1,7},{2,4},{3,5},{4,2},{5,3},{6,0},{7,1}} | collective-permute-start | bytes 1572872 | tf_op jit(solution)/shard_map/ppermute | solution.py:140
  161.0 80.0 %copy-start.16 = (bf16[8,256,128]{2,1,0:T(8,128)(2,1)}, bf16[8,256,128]{2,1,0:T(8,128)(2,1)S(1)}, u32[]{:S(2)}) copy-start(bf16[8,256,128]{2,1,0:T(8,128)(2,1)S(1)} %collective-permute-done.28.refs_1_) | copy-start | bytes 1572868
  161.0 65.0 %collective-permute-start.21 = (bf16[12,256,128]{2,1,0:T(8,128)(2,1)S(1)}, bf16[12,256,128]{2,1,0:T(8,128)(2,1)S(1)}, u32[]{:S(2)}, u32[]{:S(2)}) collective-permute-start(bf16[12,256,128]{2,1,0:T(8,128)(2,1)S(1)} %get-tuple-element.37), channel_id=1, source_target_pairs={{0,2},{1,3},{2,0},{3,1},{4,6},{5,7},{6,4},{7,5}} | collective-permute-start | bytes 2359304 | tf_op jit(solution)/shard_map/ppermute | solution.py:140
  161.8 79.2 %copy-start.17 = (bf16[8,256,128]{2,1,0:T(8,128)(2,1)}, bf16[8,256,128]{2,1,0:T(8,128)(2,1)S(1)}, u32[]{:S(2)}) copy-start(bf16[8,256,128]{2,1,0:T(8,128)(2,1)S(1)} %collective-permute-done.29.refs_2_) | copy-start | bytes 1572868
  161.8 66.2 %collective-permute-start.22 = (bf16[12,256,128]{2,1,0:T(8,128)(2,1)S(1)}, bf16[12,256,128]{2,1,0:T(8,128)(2,1)S(1)}, u32[]{:S(2)}, u32[]{:S(2)}) collective-permute-start(bf16[12,256,128]{2,1,0:T(8,128)(2,1)S(1)} %get-tuple-element.36), channel_id=1, source_target_pairs={{0,4},{1,5},{2,6},{3,7},{4,0},{5,1},{6,2},{7,3}} | collective-permute-start | bytes 2359304 | tf_op jit(solution)/shard_map/ppermute | solution.py:140
  167.9 73.1 %copy-start.18 = (bf16[8,256,128]{2,1,0:T(8,128)(2,1)}, bf16[8,256,128]{2,1,0:T(8,128)(2,1)S(1)}, u32[]{:S(2)}) copy-start(bf16[8,256,128]{2,1,0:T(8,128)(2,1)S(1)} %collective-permute-done.30.refs_3_) | copy-start | bytes 1572868
  167.9 60.9 %collective-permute-start.23 = (bf16[12,256,128]{2,1,0:T(8,128)(2,1)S(1)}, bf16[12,256,128]{2,1,0:T(8,128)(2,1)S(1)}, u32[]{:S(2)}, u32[]{:S(2)}) collective-permute-start(bf16[12,256,128]{2,1,0:T(8,128)(2,1)S(1)} %get-tuple-element.35), channel_id=1, source_target_pairs={{0,3},{1,2},{2,1},{3,0},{4,7},{5,6},{6,5},{7,4}} | collective-permute-start | bytes 2359304 | tf_op jit(solution)/shard_map/ppermute | solution.py:140
  183.1 46.3 %copy-start.19 = (bf16[8,256,128]{2,1,0:T(8,128)(2,1)}, bf16[8,256,128]{2,1,0:T(8,128)(2,1)S(1)}, u32[]{:S(2)}) copy-start(bf16[8,256,128]{2,1,0:T(8,128)(2,1)S(1)} %collective-permute-done.31.refs_4_) | copy-start | bytes 1572868
  183.1 40.9 %collective-permute-start.33 = (bf16[8,256,128]{2,1,0:T(8,128)(2,1)S(1)}, bf16[8,256,128]{2,1,0:T(8,128)(2,1)S(1)}, u32[]{:S(2)}, u32[]{:S(2)}) collective-permute-start(bf16[8,256,128]{2,1,0:T(8,128)(2,1)S(1)} %copy-done.23), channel_id=1, source_target_pairs={{0,7},{1,6},{2,5},{3,4},{4,3},{5,2},{6,1},{7,0}} | collective-permute-start | bytes 1572872 | tf_op jit(solution)/shard_map/ppermute | solution.py:140
  184.1 45.4 %copy-start.20 = (bf16[8,256,128]{2,1,0:T(8,128)(2,1)}, bf16[8,256,128]{2,1,0:T(8,128)(2,1)S(1)}, u32[]{:S(2)}) copy-start(bf16[8,256,128]{2,1,0:T(8,128)(2,1)S(1)} %collective-permute-done.32.refs_5_) | copy-start | bytes 1572868
  184.1 41.8 %collective-permute-start.34 = (bf16[8,256,128]{2,1,0:T(8,128)(2,1)S(1)}, bf16[8,256,128]{2,1,0:T(8,128)(2,1)S(1)}, u32[]{:S(2)}, u32[]{:S(2)}) collective-permute-start(bf16[8,256,128]{2,1,0:T(8,128)(2,1)S(1)} %get-tuple-element.24), channel_id=1, source_target_pairs={{0,1},{1,0},{2,3},{3,2},{4,5},{5,4},{6,7},{7,6}} | collective-permute-start | bytes 1572872 | tf_op jit(solution)/shard_map/ppermute | solution.py:140
  224.1 53.1 %collective-permute-start.24 = (bf16[12,256,128]{2,1,0:T(8,128)(2,1)}, bf16[12,256,128]{2,1,0:T(8,128)(2,1)}, u32[]{:S(2)}, u32[]{:S(2)}) collective-permute-start(bf16[12,256,128]{2,1,0:T(8,128)(2,1)} %get-tuple-element.34), channel_id=1, source_target_pairs={{0,5},{1,4},{2,7},{3,6},{4,1},{5,0},{6,3},{7,2}} | collective-permute-start | bytes 2359304 | tf_op jit(solution)/shard_map/ppermute | solution.py:140
  225.8 52.9 %collective-permute-start.25 = (bf16[12,256,128]{2,1,0:T(8,128)(2,1)}, bf16[12,256,128]{2,1,0:T(8,128)(2,1)}, u32[]{:S(2)}, u32[]{:S(2)}) collective-permute-start(bf16[12,256,128]{2,1,0:T(8,128)(2,1)} %get-tuple-element.33), channel_id=1, source_target_pairs={{0,6},{1,7},{2,4},{3,5},{4,2},{5,3},{6,0},{7,1}} | collective-permute-start | bytes 2359304 | tf_op jit(solution)/shard_map/ppermute | solution.py:140
  226.1 53.4 %collective-permute-start.26 = (bf16[12,256,128]{2,1,0:T(8,128)(2,1)}, bf16[12,256,128]{2,1,0:T(8,128)(2,1)}, u32[]{:S(2)}, u32[]{:S(2)}) collective-permute-start(bf16[12,256,128]{2,1,0:T(8,128)(2,1)} %get-tuple-element.32), channel_id=1, source_target_pairs={{0,7},{1,6},{2,5},{3,4},{4,3},{5,2},{6,1},{7,0}} | collective-permute-start | bytes 2359304 | tf_op jit(solution)/shard_map/ppermute | solution.py:140
  228.0 51.7 %collective-permute-start.27 = (bf16[12,256,128]{2,1,0:T(8,128)(2,1)}, bf16[12,256,128]{2,1,0:T(8,128)(2,1)}, u32[]{:S(2)}, u32[]{:S(2)}) collective-permute-start(bf16[12,256,128]{2,1,0:T(8,128)(2,1)} %get-tuple-element.31), channel_id=1, source_target_pairs={{0,1},{1,0},{2,3},{3,2},{4,5},{5,4},{6,7},{7,6}} | collective-permute-start | bytes 2359304 | tf_op jit(solution)/shard_map/ppermute | solution.py:140
  228.9 53.0 %collective-permute-start.14 = (bf16[12,256,128]{2,1,0:T(8,128)(2,1)}, bf16[12,256,128]{2,1,0:T(8,128)(2,1)}, u32[]{:S(2)}, u32[]{:S(2)}) collective-permute-start(bf16[12,256,128]{2,1,0:T(8,128)(2,1)} %get-tuple-element.44), channel_id=1, source_target_pairs={{0,2},{1,3},{2,0},{3,1},{4,6},{5,7},{6,4},{7,5}} | collective-permute-start | bytes 2359304 | tf_op jit(solution)/shard_map/ppermute | solution.py:140
  241.1 41.8 %copy-start.35 = (bf16[1,4,5,32,128]{4,2,0,3,1:T(8,128)(2,1)S(1)}, bf16[1,4,5,32,128]{4,2,0,3,1:T(8,128)(2,1)}, u32[]{:S(2)}) copy-start(bf16[1,4,5,32,128]{4,2,0,3,1:T(8,128)(2,1)} %copy-done.34) | copy-start | bytes 491524
  277.2 20.7 %collective-permute-start.15 = (bf16[12,256,128]{2,1,0:T(8,128)(2,1)}, bf16[12,256,128]{2,1,0:T(8,128)(2,1)}, u32[]{:S(2)}, u32[]{:S(2)}) collective-permute-start(bf16[12,256,128]{2,1,0:T(8,128)(2,1)} %get-tuple-element.43), channel_id=1, source_target_pairs={{0,4},{1,5},{2,6},{3,7},{4,0},{5,1},{6,2},{7,3}} | collective-permute-start | bytes 2359304 | tf_op jit(solution)/shard_map/ppermute | solution.py:140
  278.7 19.4 %collective-permute-start.16 = (bf16[12,256,128]{2,1,0:T(8,128)(2,1)}, bf16[12,256,128]{2,1,0:T(8,128)(2,1)}, u32[]{:S(2)}, u32[]{:S(2)}) collective-permute-start(bf16[12,256,128]{2,1,0:T(8,128)(2,1)} %get-tuple-element.42), channel_id=1, source_target_pairs={{0,3},{1,2},{2,1},{3,0},{4,7},{5,6},{6,5},{7,4}} | collective-permute-start | bytes 2359304 | tf_op jit(solution)/shard_map/ppermute | solution.py:140
  279.5 68.9 %collective-permute-start.17 = (bf16[12,256,128]{2,1,0:T(8,128)(2,1)}, bf16[12,256,128]{2,1,0:T(8,128)(2,1)}, u32[]{:S(2)}, u32[]{:S(2)}) collective-permute-start(bf16[12,256,128]{2,1,0:T(8,128)(2,1)} %get-tuple-element.41), channel_id=1, source_target_pairs={{0,5},{1,4},{2,7},{3,6},{4,1},{5,0},{6,3},{7,2}} | collective-permute-start | bytes 2359304 | tf_op jit(solution)/shard_map/ppermute | solution.py:140
  279.7 70.2 %collective-permute-start.18 = (bf16[12,256,128]{2,1,0:T(8,128)(2,1)}, bf16[12,256,128]{2,1,0:T(8,128)(2,1)}, u32[]{:S(2)}, u32[]{:S(2)}) collective-permute-start(bf16[12,256,128]{2,1,0:T(8,128)(2,1)} %get-tuple-element.40), channel_id=1, source_target_pairs={{0,6},{1,7},{2,4},{3,5},{4,2},{5,3},{6,0},{7,1}} | collective-permute-start | bytes 2359304 | tf_op jit(solution)/shard_map/ppermute | solution.py:140
  281.9 67.9 %collective-permute-start.19 = (bf16[12,256,128]{2,1,0:T(8,128)(2,1)}, bf16[12,256,128]{2,1,0:T(8,128)(2,1)}, u32[]{:S(2)}, u32[]{:S(2)}) collective-permute-start(bf16[12,256,128]{2,1,0:T(8,128)(2,1)} %get-tuple-element.39), channel_id=1, source_target_pairs={{0,7},{1,6},{2,5},{3,4},{4,3},{5,2},{6,1},{7,0}} | collective-permute-start | bytes 2359304 | tf_op jit(solution)/shard_map/ppermute | solution.py:140
  297.9 73.2 %collective-permute-start.20 = (bf16[12,256,128]{2,1,0:T(8,128)(2,1)}, bf16[12,256,128]{2,1,0:T(8,128)(2,1)S(1)}, u32[]{:S(2)}, u32[]{:S(2)}) collective-permute-start(bf16[12,256,128]{2,1,0:T(8,128)(2,1)} %get-tuple-element.38), channel_id=1, source_target_pairs={{0,1},{1,0},{2,3},{3,2},{4,5},{5,4},{6,7},{7,6}} | collective-permute-start | bytes 2359304 | tf_op jit(solution)/shard_map/ppermute | solution.py:140
  298.1 74.8 %collective-permute-start.42 = (bf16[12,256,128]{2,1,0:T(8,128)(2,1)}, bf16[12,256,128]{2,1,0:T(8,128)(2,1)S(1)}, u32[]{:S(2)}, u32[]{:S(2)}) collective-permute-start(bf16[12,256,128]{2,1,0:T(8,128)(2,1)} %get-tuple-element.16), channel_id=1, source_target_pairs={{0,2},{1,3},{2,0},{3,1},{4,6},{5,7},{6,4},{7,5}} | collective-permute-start | bytes 2359304 | tf_op jit(solution)/shard_map/ppermute | solution.py:140
  348.3 26.1 %collective-permute-start.43 = (bf16[12,256,128]{2,1,0:T(8,128)(2,1)}, bf16[12,256,128]{2,1,0:T(8,128)(2,1)S(1)}, u32[]{:S(2)}, u32[]{:S(2)}) collective-permute-start(bf16[12,256,128]{2,1,0:T(8,128)(2,1)} %get-tuple-element.15), channel_id=1, source_target_pairs={{0,4},{1,5},{2,6},{3,7},{4,0},{5,1},{6,2},{7,3}} | collective-permute-start | bytes 2359304 | tf_op jit(solution)/shard_map/ppermute | solution.py:140
  349.8 24.8 %collective-permute-start.44 = (bf16[12,256,128]{2,1,0:T(8,128)(2,1)}, bf16[12,256,128]{2,1,0:T(8,128)(2,1)S(1)}, u32[]{:S(2)}, u32[]{:S(2)}) collective-permute-start(bf16[12,256,128]{2,1,0:T(8,128)(2,1)} %get-tuple-element.14), channel_id=1, source_target_pairs={{0,3},{1,2},{2,1},{3,0},{4,7},{5,6},{6,5},{7,4}} | collective-permute-start | bytes 2359304 | tf_op jit(solution)/shard_map/ppermute | solution.py:140
  349.8 35.1 %collective-permute-start.45 = (bf16[12,256,128]{2,1,0:T(8,128)(2,1)}, bf16[12,256,128]{2,1,0:T(8,128)(2,1)S(1)}, u32[]{:S(2)}, u32[]{:S(2)}) collective-permute-start(bf16[12,256,128]{2,1,0:T(8,128)(2,1)} %get-tuple-element.13), channel_id=1, source_target_pairs={{0,5},{1,4},{2,7},{3,6},{4,1},{5,0},{6,3},{7,2}} | collective-permute-start | bytes 2359304 | tf_op jit(solution)/shard_map/ppermute | solution.py:140
  371.2 82.6 %collective-permute-start.49 = (bf16[14,256,128]{2,1,0:T(8,128)(2,1)}, bf16[14,256,128]{2,1,0:T(8,128)(2,1)}, u32[]{:S(2)}, u32[]{:S(2)}) collective-permute-start(bf16[14,256,128]{2,1,0:T(8,128)(2,1)} %get-tuple-element.8), channel_id=1, source_target_pairs={{0,2},{1,3},{2,0},{3,1},{4,6},{5,7},{6,4},{7,5}} | collective-permute-start | bytes 2752520 | tf_op jit(solution)/shard_map/ppermute | solution.py:140
  372.9 82.3 %collective-permute-start.50 = (bf16[14,256,128]{2,1,0:T(8,128)(2,1)}, bf16[14,256,128]{2,1,0:T(8,128)(2,1)}, u32[]{:S(2)}, u32[]{:S(2)}) collective-permute-start(bf16[14,256,128]{2,1,0:T(8,128)(2,1)} %get-tuple-element.7), channel_id=1, source_target_pairs={{0,4},{1,5},{2,6},{3,7},{4,0},{5,1},{6,2},{7,3}} | collective-permute-start | bytes 2752520 | tf_op jit(solution)/shard_map/ppermute | solution.py:140
  374.4 75.9 %collective-permute-start.46 = (bf16[12,256,128]{2,1,0:T(8,128)(2,1)}, bf16[12,256,128]{2,1,0:T(8,128)(2,1)}, u32[]{:S(2)}, u32[]{:S(2)}) collective-permute-start(bf16[12,256,128]{2,1,0:T(8,128)(2,1)} %get-tuple-element.12), channel_id=1, source_target_pairs={{0,6},{1,7},{2,4},{3,5},{4,2},{5,3},{6,0},{7,1}} | collective-permute-start | bytes 2359304 | tf_op jit(solution)/shard_map/ppermute | solution.py:140
  374.7 76.4 %collective-permute-start.47 = (bf16[12,256,128]{2,1,0:T(8,128)(2,1)}, bf16[12,256,128]{2,1,0:T(8,128)(2,1)}, u32[]{:S(2)}, u32[]{:S(2)}) collective-permute-start(bf16[12,256,128]{2,1,0:T(8,128)(2,1)} %get-tuple-element.11), channel_id=1, source_target_pairs={{0,7},{1,6},{2,5},{3,4},{4,3},{5,2},{6,1},{7,0}} | collective-permute-start | bytes 2359304 | tf_op jit(solution)/shard_map/ppermute | solution.py:140
  384.9 67.4 %collective-permute-start.48 = (bf16[12,256,128]{2,1,0:T(8,128)(2,1)}, bf16[12,256,128]{2,1,0:T(8,128)(2,1)}, u32[]{:S(2)}, u32[]{:S(2)}) collective-permute-start(bf16[12,256,128]{2,1,0:T(8,128)(2,1)} %get-tuple-element.10), channel_id=1, source_target_pairs={{0,1},{1,0},{2,3},{3,2},{4,5},{5,4},{6,7},{7,6}} | collective-permute-start | bytes 2359304 | tf_op jit(solution)/shard_map/ppermute | solution.py:140
  386.0 69.3 %copy-start.3 = (f32[4,32,5120]{2,1,0:T(8,128)S(1)}, f32[4,32,5120]{2,1,0:T(8,128)}, u32[]{:S(2)}) copy-start(f32[4,32,5120]{2,1,0:T(8,128)} %get-tuple-element.73) | copy-start | bytes 7864324
  450.3 65.5 %collective-permute-start.51 = (bf16[14,256,128]{2,1,0:T(8,128)(2,1)}, bf16[14,256,128]{2,1,0:T(8,128)(2,1)}, u32[]{:S(2)}, u32[]{:S(2)}) collective-permute-start(bf16[14,256,128]{2,1,0:T(8,128)(2,1)} %get-tuple-element.6), channel_id=1, source_target_pairs={{0,3},{1,2},{2,1},{3,0},{4,7},{5,6},{6,5},{7,4}} | collective-permute-start | bytes 2752520 | tf_op jit(solution)/shard_map/ppermute | solution.py:140
  451.1 66.2 %collective-permute-start.52 = (bf16[14,256,128]{2,1,0:T(8,128)(2,1)}, bf16[14,256,128]{2,1,0:T(8,128)(2,1)}, u32[]{:S(2)}, u32[]{:S(2)}) collective-permute-start(bf16[14,256,128]{2,1,0:T(8,128)(2,1)} %get-tuple-element.5), channel_id=1, source_target_pairs={{0,5},{1,4},{2,7},{3,6},{4,1},{5,0},{6,3},{7,2}} | collective-permute-start | bytes 2752520 | tf_op jit(solution)/shard_map/ppermute | solution.py:140
  452.3 65.3 %collective-permute-start.53 = (bf16[14,256,128]{2,1,0:T(8,128)(2,1)}, bf16[14,256,128]{2,1,0:T(8,128)(2,1)}, u32[]{:S(2)}, u32[]{:S(2)}) collective-permute-start(bf16[14,256,128]{2,1,0:T(8,128)(2,1)} %get-tuple-element.4), channel_id=1, source_target_pairs={{0,6},{1,7},{2,4},{3,5},{4,2},{5,3},{6,0},{7,1}} | collective-permute-start | bytes 2752520 | tf_op jit(solution)/shard_map/ppermute | solution.py:140
  453.8 65.3 %collective-permute-start.54 = (bf16[14,256,128]{2,1,0:T(8,128)(2,1)}, bf16[14,256,128]{2,1,0:T(8,128)(2,1)}, u32[]{:S(2)}, u32[]{:S(2)}) collective-permute-start(bf16[14,256,128]{2,1,0:T(8,128)(2,1)} %get-tuple-element.9), channel_id=1, source_target_pairs={{0,7},{1,6},{2,5},{3,4},{4,3},{5,2},{6,1},{7,0}} | collective-permute-start | bytes 2752520 | tf_op jit(solution)/shard_map/ppermute | solution.py:140
  455.2 65.0 %collective-permute-start.55 = (bf16[14,256,128]{2,1,0:T(8,128)(2,1)}, bf16[14,256,128]{2,1,0:T(8,128)(2,1)}, u32[]{:S(2)}, u32[]{:S(2)}) collective-permute-start(bf16[14,256,128]{2,1,0:T(8,128)(2,1)} %get-tuple-element.3), channel_id=1, source_target_pairs={{0,1},{1,0},{2,3},{3,2},{4,5},{5,4},{6,7},{7,6}} | collective-permute-start | bytes 2752520 | tf_op jit(solution)/shard_map/ppermute | solution.py:140
  515.8 112.4 %collective-permute-start.37 = (bf16[6,256,128]{2,1,0:T(8,128)(2,1)}, bf16[6,256,128]{2,1,0:T(8,128)(2,1)S(1)}, u32[]{:S(2)}, u32[]{:S(2)}) collective-permute-start(bf16[6,256,128]{2,1,0:T(8,128)(2,1)} %get-tuple-element.21), channel_id=1, source_target_pairs={{0,3},{1,2},{2,1},{3,0},{4,7},{5,6},{6,5},{7,4}} | collective-permute-start | bytes 1179656 | tf_op jit(solution)/shard_map/ppermute | solution.py:140
  517.3 111.0 %collective-permute-start.38 = (bf16[6,256,128]{2,1,0:T(8,128)(2,1)}, bf16[6,256,128]{2,1,0:T(8,128)(2,1)S(1)}, u32[]{:S(2)}, u32[]{:S(2)}) collective-permute-start(bf16[6,256,128]{2,1,0:T(8,128)(2,1)} %get-tuple-element.20), channel_id=1, source_target_pairs={{0,5},{1,4},{2,7},{3,6},{4,1},{5,0},{6,3},{7,2}} | collective-permute-start | bytes 1179656 | tf_op jit(solution)/shard_map/ppermute | solution.py:140
  517.6 110.7 %collective-permute-start.39 = (bf16[6,256,128]{2,1,0:T(8,128)(2,1)}, bf16[6,256,128]{2,1,0:T(8,128)(2,1)}, u32[]{:S(2)}, u32[]{:S(2)}) collective-permute-start(bf16[6,256,128]{2,1,0:T(8,128)(2,1)} %get-tuple-element.19), channel_id=1, source_target_pairs={{0,6},{1,7},{2,4},{3,5},{4,2},{5,3},{6,0},{7,1}} | collective-permute-start | bytes 1179656 | tf_op jit(solution)/shard_map/ppermute | solution.py:140
  519.1 109.3 %collective-permute-start.40 = (bf16[6,256,128]{2,1,0:T(8,128)(2,1)}, bf16[6,256,128]{2,1,0:T(8,128)(2,1)}, u32[]{:S(2)}, u32[]{:S(2)}) collective-permute-start(bf16[6,256,128]{2,1,0:T(8,128)(2,1)} %get-tuple-element.18), channel_id=1, source_target_pairs={{0,7},{1,6},{2,5},{3,4},{4,3},{5,2},{6,1},{7,0}} | collective-permute-start | bytes 1179656 | tf_op jit(solution)/shard_map/ppermute | solution.py:140
  520.2 108.2 %collective-permute-start.41 = (bf16[6,256,128]{2,1,0:T(8,128)(2,1)}, bf16[6,256,128]{2,1,0:T(8,128)(2,1)}, u32[]{:S(2)}, u32[]{:S(2)}) collective-permute-start(bf16[6,256,128]{2,1,0:T(8,128)(2,1)} %get-tuple-element.17), channel_id=1, source_target_pairs={{0,1},{1,0},{2,3},{3,2},{4,5},{5,4},{6,7},{7,6}} | collective-permute-start | bytes 1179656 | tf_op jit(solution)/shard_map/ppermute | solution.py:140
  (37 other events, 424.9 us)
